TPU v7x, 128 devices: a whole 4x4x4 slice. The times are simulated.
128 devices in a mesh: seq: 16 (over x_lo, z, core), head: 4 (over y), batch: 2 (over x_hi).
Axes of the slice: x: 4 (x_hi: 2, x_lo: 2; x = x_hi * 2 + x_lo), y: 4, z: 4, core: 2. Of those that a mesh axis runs over, the one named last changes fastest.
Arguments:
- tokens: bfloat16 [32768, 2048], P(('batch', 'seq')), parts along dimension 0, may hold values from -6 to 6
- neighbor_bank: bfloat16 [512, 256, 2048], P(('batch', 'seq')), parts along dimension 0, may hold values from -2100 to 2100
- slots: int32 [512], P(('batch', 'seq')), parts along dimension 0, may hold values from 0 to 15
- w_query: bfloat16 [2048, 2048], P('seq', 'head'), may hold values from -0.125 to 0.125
- w_key: bfloat16 [2048, 2048], P('seq', 'head'), may hold values from -0.125 to 0.125
- w_value: bfloat16 [2048, 2048], P('seq', 'head'), may hold values from -0.125 to 0.125
- w_out: bfloat16 [2048, 2048], P('head', 'seq'), may hold values from -0.125 to 0.125
Outputs:
- cross_out: bfloat16 [32768, 2048], P(('batch', 'seq'), 'head'), parts along dimension 0
There are 2 independent parts, one for each index of `batch`. A program takes and returns all parts, laid end to end along the dimension named above; an argument that names none is the same for every part. Nothing has to cross between parts.
Inputs may be any that keep to these rules, and one draw needn't show every extreme that they name: Entry c picks row c // 16 * 16 + slots[c] of neighbor_bank.
All inputs are finite; a program needn't handle non-finite values.
Results may differ from a plain program's by a relative error of at most 0.006.
The roundings to bfloat16 on the way count: a program that leaves them out, or rounds other values in their place, can miss the bound.
Values may be sent and summed in bfloat16 or wider, within the bound.
A program may use at most 128 MiB of HBM per device.

v0:
```python
import math

import jax
import jax.numpy as jnp
from jax import lax
from jax.sharding import PartitionSpec as P

HEAD_DIM = 128


def passed_along(block, axis, distance):
    devices = range(lax.axis_size(axis))
    route = [(i - distance, i) for i in devices if i - distance in devices]
    return lax.ppermute(block, axis, route)


def side_by_side(arrays, axis, dim, along):
    ends, at = ([], 0)
    for a in arrays[:-1]:
        at += a.shape[along]
        ends.append(at)
    both = jnp.concatenate(arrays, axis=along)
    return tuple(jnp.split(lax.all_gather(both, axis, axis=dim, tiled=True), ends, axis=along))


def attend(query_blocks, key_blocks, value_blocks):
    scores = jnp.einsum(
        "cmhd,cnhd->chmn", query_blocks, key_blocks, preferred_element_type=jnp.float32
    ) / math.sqrt(HEAD_DIM)
    peak_score = jnp.max(scores, axis=-1, keepdims=True)
    exponent = jnp.exp(scores - peak_score)
    weights = (exponent / jnp.sum(exponent, axis=-1, keepdims=True)).astype(jnp.bfloat16)
    blended = jnp.einsum(
        "chmn,cnhd->cmhd", weights, value_blocks, preferred_element_type=jnp.float32
    ).astype(jnp.bfloat16)
    return blended.reshape(blended.shape[0] * blended.shape[1], blended.shape[2] * blended.shape[3])


def fold_rows(source, shard_rows):
    return jnp.dot(source, shard_rows, preferred_element_type=jnp.float32)


def local(tokens, neighbor_bank, slots, w_query, w_key, w_value, w_out):
    tok_rows, model_width = tokens.shape
    block_count = neighbor_bank.shape[0]
    neighbor_rows = neighbor_bank.shape[1]
    block_len = tok_rows // block_count
    local_width = w_query.shape[1]
    local_heads = local_width // HEAD_DIM
    hidden = tokens.astype(jnp.float32)
    normed = (hidden * lax.rsqrt(jnp.mean(hidden * hidden, axis=-1, keepdims=True) + 1e-06)).astype(
        jnp.bfloat16
    )
    retrieved = jnp.take(neighbor_bank, slots, axis=0)
    arrived = passed_along(retrieved[block_count - 1], "seq", 1)
    context = jnp.concatenate([arrived[None], retrieved[: block_count - 1]], axis=0)
    context_flat = context.reshape(block_count * neighbor_rows, model_width)
    shard_rows = side_by_side((w_query, w_key, w_value), "seq", 0, 1)
    query_sum = fold_rows(normed, shard_rows[0])
    key_sum = fold_rows(context_flat, shard_rows[1])
    value_sum = fold_rows(context_flat, shard_rows[2])
    query_blocks = query_sum.astype(jnp.bfloat16).reshape(
        block_count, block_len, local_heads, HEAD_DIM
    )
    key_blocks = key_sum.astype(jnp.bfloat16).reshape(
        block_count, neighbor_rows, local_heads, HEAD_DIM
    )
    value_blocks = value_sum.astype(jnp.bfloat16).reshape(
        block_count, neighbor_rows, local_heads, HEAD_DIM
    )
    attended = attend(query_blocks, key_blocks, value_blocks)
    every_head = lax.all_gather(attended, "head", axis=1, tiled=True)
    wide_rows = lax.all_gather(w_out, "seq", axis=1, tiled=True)
    own_columns = lax.all_to_all(wide_rows, "head", split_axis=1, concat_axis=0, tiled=True)
    return jnp.dot(every_head, own_columns, preferred_element_type=jnp.float32).astype(jnp.bfloat16)


def solution(mesh):
    in_specs = (
        P(("batch", "seq"), None),
        P(("batch", "seq"), None, None),
        P(("batch", "seq")),
        P("seq", "head"),
        P("seq", "head"),
        P("seq", "head"),
        P("head", "seq"),
    )
    out_specs = P(("batch", "seq"), "head")
    return jax.shard_map(local, mesh=mesh, in_specs=in_specs, out_specs=out_specs, check_vma=False)
```

profile of v0, /device:TPU:3, one launch (start us, length us, event | category | flops | bytes accessed | tf_op | source)
XLA Modules:
  0.0 214.9 jit_solution(9233872285534013376)
XLA Ops:
  6.5 0.0 all-gather.4.cloned.1.call-start
  6.5 1.8 pad_maximum_fusion.1
  8.3 0.0 all-gather.4.cloned.1.call-update
  8.4 0.0 all-gather.8.cloned.1.call-start
  8.4 0.7 compare_select_fusion
  9.1 0.0 copy-start.4
  9.1 13.1 %gather_fusion = bf16[16,256,2048]{2,1,0:T(8,128)(2,1)} fusion(bf16[16,256,2048]{2,1,0:T(8,128)(2,1)} %param.8, s32[1024]{0:T(1024)S(1)} %pad_clamp_fusion), kind=kCustom, calls=%fused_computation | custom fusion | bytes 33554496 | tf_op jit(solution)/shard_map/jit(_take)/gather | solution.py:54
  22.2 0.0 copy-done.4
  22.2 0.0 copy-start.3
  22.2 8.8 %broadcast_select_fusion = bf16[16,256,2048]{2,1,0:T(8,128)(2,1)S(1)} fusion(bf16[16,256,2048]{2,1,0:T(8,128)(2,1)} %gather_fusion, pred[16]{0:T(512)(128)(4,1)S(1)} %compare_and_fusion), kind=kLoop, calls=%fused_computation.3 | loop fusion | flops 8388608 | bytes 33554448 | tf_op jit(solution)/shard_map/jit(_take)/select_n | solution.py:54
  30.9 0.0 copy-start
  30.9 5.9 %copy-done = bf16[16,256,2048]{2,1,0:T(8,128)(2,1)} copy-done((bf16[16,256,2048]{2,1,0:T(8,128)(2,1)}, bf16[16,256,2048]{2,1,0:T(8,128)(2,1)S(1)}, u32[]{:S(2)}) %copy-start) | copy-done | bytes 16777240
  36.9 0.1 slice_bitcast_fusion
  37.0 4.2 %collective-permute-start = (bf16[256,2048]{1,0:T(8,128)(2,1)S(1)}, bf16[256,2048]{1,0:T(8,128)(2,1)S(1)}, u32[]{:S(2)}, u32[]{:S(2)}) collective-permute-start(bf16[256,2048]{1,0:T(8,128)(2,1)S(1)} %slice_bitcast_fusion), channel_id=1, source_target_pairs={{0,8},{8,16},{16,24},{24,32},{32,40},{40,48},{48,56},{56,64},{64,7... | collective-permute-start | bytes 3145736 | tf_op jit(solution)/shard_map/ppermute | solution.py:14
  41.1 0.0 copy-done.3
  41.1 0.8 copy.19
  41.9 0.0 all-gather.8.cloned.1.call-update
  41.9 0.0 all-gather.6.cloned.1.call-start
  42.0 0.0 copy-start.1
  42.0 0.0 slice-start
  42.0 2.2 %copy-done.1 = bf16[1024,2048]{1,0:T(8,128)(2,1)S(1)} copy-done((bf16[1024,2048]{1,0:T(8,128)(2,1)S(1)}, bf16[1024,2048]{1,0:T(8,128)(2,1)}, u32[]{:S(2)}) %copy-start.1) | copy-done | bytes 4194328
  44.2 0.9 fusion.1
  45.1 16.4 %collective-permute-done = bf16[256,2048]{1,0:T(8,128)(2,1)S(1)} collective-permute-done((bf16[256,2048]{1,0:T(8,128)(2,1)S(1)}, bf16[256,2048]{1,0:T(8,128)(2,1)S(1)}, u32[]{:S(2)}, u32[]{:S(2)}) %collective-permute-start) | collective-permute-done | bytes 1048608 | tf_op jit(solution)/shard_map/ppermute | solution.py:14
  61.5 0.0 slice-done
  61.5 6.4 %pad_maximum_fusion = bf16[16,256,2048]{2,1,0:T(8,128)(2,1)} fusion(bf16[15,256,2048]{2,1,0:T(8,128)(2,1)S(1)} %slice-done, bf16[1,256,2048]{2,1,0:T(8,128)(2,1)S(1)} %bitcast.25), kind=kLoop, calls=%fused_computation.2 | loop fusion | flops 8388608 | bytes 33554432 | tf_op jit(solution)/shard_map/concatenate | solution.py:56
  68.0 0.0 all-gather.4.cloned.1.call-done
  68.0 14.5 %convolution_convert_fusion = bf16[4096,512]{1,0:T(8,128)(2,1)} fusion(bf16[4096,2048]{1,0:T(8,128)(2,1)} %bitcast.18, bf16[2048,1536]{1,0:T(8,128)(2,1)} %all-gather.4.cloned.1.call-done), kind=kOutput, calls=%fused_computation.8 | convolution fusion | flops 8592031744 | bytes 23068672 | tf_op jit(solution)/shard_map/dot_general | solution.py:40
  82.4 7.0 %reshape.36 = bf16[16,256,4,128]{3,2,1,0:T(4,128)(2,1)} reshape(bf16[4096,512]{1,0:T(8,128)(2,1)} %convolution_convert_fusion) | data formatting | bytes 8388608 | tf_op jit(solution)/shard_map/reshape | solution.py:65
  89.4 5.2 %fusion.21 = bf16[1024,512]{1,0:T(8,128)(2,1)S(1)} fusion(bf16[2048,1536]{1,0:T(8,128)(2,1)} %all-gather.4.cloned.1.call-done, bf16[1024,2048]{1,0:T(8,128)(2,1)} %param.7, f32[1024]{0:T(1024)S(1)} %add_rsqrt_fusion), kind=kOutput, calls=%fused_computation.26 | convolution fusion | flops 2154299392 | bytes 7344128 | tf_op jit(solution)/shard_map/dot_general | solution.py:40
  94.6 0.3 reshape.35
  94.9 14.4 %convolution_convert_fusion.1 = bf16[4096,512]{1,0:T(8,128)(2,1)} fusion(bf16[4096,2048]{1,0:T(8,128)(2,1)} %bitcast.19, bf16[2048,1536]{1,0:T(8,128)(2,1)} %all-gather.4.cloned.1.call-done), kind=kOutput, calls=%fused_computation.9 | convolution fusion | flops 8592031744 | bytes 23068672 | tf_op jit(solution)/shard_map/dot_general | solution.py:40
  109.3 6.9 %reshape.34 = bf16[16,256,4,128]{3,2,1,0:T(4,128)(2,1)} reshape(bf16[4096,512]{1,0:T(8,128)(2,1)} %convolution_convert_fusion.1) | data formatting | bytes 8388608 | tf_op jit(solution)/shard_map/reshape | solution.py:68
  116.2 3.8 %fusion.7 = f32[16,4,64,256]{3,2,1,0:T(8,128)S(1)} fusion(bf16[16,256,4,128]{3,2,1,0:T(4,128)(2,1)} %reshape.36, bf16[16,64,4,128]{3,2,1,0:T(4,128)(2,1)S(1)} %reshape.35), kind=kOutput, calls=%fused_computation.13 | convolution fusion | flops 268435456 | bytes 9437184 | tf_op jit(solution)/shard_map/cmhd,cnhd->chmn/dot_general | solution.py:27
  120.0 0.0 copy-start.2
  120.0 2.0 copy-done.2
  121.9 1.6 fusion.38
  123.6 11.9 %fusion.26 = bf16[16,64,4,128]{3,1,2,0:T(8,128)(2,1)S(1)} fusion(bf16[16,256,4,128]{3,2,1,0:T(4,128)(2,1)} %reshape.34, f32[16,4,64]{2,1,0:T(4,128)S(1)} %fusion.38, f32[16,4,64,256]{3,2,1,0:T(8,128)} %copy-done.2), kind=kOutput, calls=%fused_computation.28 | convolution fusion | flops 274206976 | bytes 9453568 | tf_op jit(solution)/shard_map/chmn,cnhd->cmhd/dot_general | solution.py:33
  135.5 0.9 copy.18
  136.4 1.2 copy.33
  137.5 0.0 all-gather.6.cloned.1.call-update
  137.6 0.0 all-gather.8.cloned.1.call-done
  137.6 35.8 %all_to_all.19 = bf16[512,4,512]{0,2,1:T(8,128)(2,1)S(1)} all-to-all(bf16[512,4,512]{0,2,1:T(8,128)(2,1)} %bitcast.23), channel_id=1, replica_groups=mesh['seq'=16,'head'=4,'batch'=2] {'head'}, dimensions={1} | all-to-all | bytes 4194304 | tf_op jit(solution)/shard_map/all_to_all | solution.py:74
  173.4 2.4 %copy.20 = bf16[4,512,512]{2,1,0:T(8,128)(2,1)} copy(bf16[4,512,512]{1,2,0:T(8,128)(2,1)S(1)} %bitcast.20) | data formatting | bytes 4194304 | tf_op jit(solution)/shard_map/all_to_all | solution.py:74
  175.8 26.4 %all-gather.6.cloned.1.call-done = bf16[1024,2048]{1,0:T(8,128)(2,1)} async-done(((bf16[1024,512]{1,0:T(8,128)(2,1)}), bf16[1024,2048]{1,0:T(8,128)(2,1)}) %all-gather.6.cloned.1.call-update) | async-done | bytes 4194320 | tf_op jit(solution)/shard_map/all_gather | solution.py:72
  202.2 6.2 %convolution_convert_fusion.2 = bf16[1024,512]{1,0:T(8,128)(2,1)} fusion(bf16[1024,2048]{1,0:T(8,128)(2,1)} %all-gather.6.cloned.1.call-done, bf16[2048,512]{1,0:T(8,128)(2,1)} %bitcast.24), kind=kOutput, calls=%fused_computation.27 | convolution fusion | flops 2148007936 | bytes 7340032 | tf_op jit(solution)/shard_map/dot_general | solution.py:75
  (3 shorter events, 0.0 us)
Async XLA Ops:
  6.5 61.4 %all-gather.4.cloned.1.call-start = ((), (), s32[]{:S(2)}) async-start(), calls=%async_computation.1 | async-start | bytes 6684672 | tf_op jit(solution)/shard_map/all_gather | solution.py:23
  8.4 129.2 %all-gather.8.cloned.1.call-start = ((), (), s32[]{:S(2)}) async-start(), calls=%async_computation.3 | async-start | bytes 2228224 | tf_op jit(solution)/shard_map/all_gather | solution.py:73
  9.1 13.1 %copy-start.4 = (s32[16]{0:T(128)S(1)}, s32[16]{0:T(128)}, u32[]{:S(2)}) copy-start(s32[16]{0:T(128)} %param.9) | copy-start | bytes 196
  22.2 19.0 %copy-start.3 = (bf16[512,128]{1,0:T(8,128)(2,1)S(1)}, bf16[512,128]{1,0:T(8,128)(2,1)}, u32[]{:S(2)}) copy-start(bf16[512,128]{1,0:T(8,128)(2,1)} %param.13) | copy-start | bytes 393220
  30.9 5.9 %copy-start = (bf16[16,256,2048]{2,1,0:T(8,128)(2,1)}, bf16[16,256,2048]{2,1,0:T(8,128)(2,1)S(1)}, u32[]{:S(2)}) copy-start(bf16[16,256,2048]{2,1,0:T(8,128)(2,1)S(1)} %broadcast_select_fusion) | copy-start | bytes 50331652
  37.0 24.6 %collective-permute-start = (bf16[256,2048]{1,0:T(8,128)(2,1)S(1)}, bf16[256,2048]{1,0:T(8,128)(2,1)S(1)}, u32[]{:S(2)}, u32[]{:S(2)}) collective-permute-start(bf16[256,2048]{1,0:T(8,128)(2,1)S(1)} %slice_bitcast_fusion), channel_id=1, source_target_pairs={{0,8},{8,16},{16,24},{24,32},{32,40},{40,48},{48,56},{56,64},{64,7... | collective-permute-start | bytes 3145736 | tf_op jit(solution)/shard_map/ppermute | solution.py:14
  41.9 160.2 %all-gather.6.cloned.1.call-start = ((), (), s32[]{:S(2)}) async-start(), calls=%async_computation.2 | async-start | bytes 5242880 | tf_op jit(solution)/shard_map/all_gather | solution.py:72
  42.0 2.3 %copy-start.1 = (bf16[1024,2048]{1,0:T(8,128)(2,1)S(1)}, bf16[1024,2048]{1,0:T(8,128)(2,1)}, u32[]{:S(2)}) copy-start(bf16[1024,2048]{1,0:T(8,128)(2,1)} %param.7) | copy-start | bytes 12582916
  42.0 19.5 %slice-start = ((bf16[16,256,2048]{2,1,0:T(8,128)(2,1)}), bf16[15,256,2048]{2,1,0:T(8,128)(2,1)S(1)}, s32[]{:S(2)}) async-start(bf16[16,256,2048]{2,1,0:T(8,128)(2,1)} %copy-done), calls=%async_computation.4 | async-start | bytes 31457280 | tf_op jit(solution)/shard_map/slice | solution.py:56
  120.0 2.0 copy-start.2
Sparse Core Ops, SparseCore 0:
  9.0 46.2 all-gather.3
  57.0 37.5 all-gather.7
  137.7 64.4 all-gather.5
where the time goes:
time: 215 us
  matrix products  55.9 us (26%)
  waiting for transfers between devices  42.8 us (20%)
  local copies, waits for them, and re-layouts  42.6 us (20%)
  blocking collectives  35.8 us (17%)
  other arithmetic  20.2 us (9%)
  between operations  13.2 us (6%)
  starting transfers between devices  4.26 us (2%)
    all_to_all x1, blocking collectives, local(): lax.all_to_all(wide_rows, 'head', split_axis=1, concat_axis=0, tiled=True)  35.8 us
    dot_general x3, matrix products, fold_rows(): return jnp.dot(source, shard_rows, preferred_element_type=jnp.float32)  34.1 us
    all_gather x1, waiting for transfers between devices, local(): every_head = lax.all_gather(attended, 'head', axis=1, tiled=True)  26.4 us
    ppermute x1, waiting for transfers between devices, passed_along(): return lax.ppermute(block, axis, route)  16.4 us
    gather x1, local copies, waits for them, and re-layouts, local(): retrieved = jnp.take(neighbor_bank, slots, axis=0)  13.1 us
    unnamed x12, local copies, waits for them, and re-layouts  12.1 us
    dot_general x1, matrix products, attend(): jnp.einsum('chmn,cnhd->cmhd', weights, value_blocks, preferred_element_ty...  11.9 us
    select_n x2, other arithmetic, local(): retrieved = jnp.take(neighbor_bank, slots, axis=0)  9.41 us
  transfers between devices with their start and end apart: 4, of which 2 were waited for; matrix products, arithmetic and copies ran while one was open for 47% of the time, Pallas kernels for 0%

commit v1 on v0

v1 whole, which is shorter than its diff:
```python
import functools
import math

import jax
import jax.numpy as jnp
from jax import lax
from jax.experimental import pallas as pl
from jax.experimental.pallas import tpu as pltpu
from jax.sharding import PartitionSpec as P

MESH = pl.DeviceIdType.MESH
HEAD_DIM = 128
BLOCKS = 16
BLOCK = 64
KEYS = 256
D = 2048
ROWS = BLOCKS * BLOCK
HEADS = 4
GROUPS = 2
GROUP_ROWS = ROWS // GROUPS
SCALE = 1.0 / math.sqrt(HEAD_DIM)
BF16 = jnp.bfloat16
F32 = jnp.float32


def kernel(
    tokens,
    bank_hbm,
    slots,
    w_query,
    w_key,
    w_value,
    w_out,
    out,
    normed,
    bank,
    w_all,
    o_all,
    queries,
    kv_pairs,
    kv_send,
    kv_recv,
    attended,
    total,
    stage_sem,
    load_sem,
    w_send,
    w_recv,
    y_send,
    y_recv,
    kv_send_sem,
    kv_recv_sem,
    perm_sem,
):
    seq = lax.axis_index("seq")
    y = lax.axis_index("head")
    half = lax.axis_index("batch")
    p = lax.div(seq, 8)
    z = lax.rem(lax.div(seq, 2), 4)
    c = lax.rem(seq, 2)
    z_next = lax.rem(z + 1, 4)
    z_prev = lax.rem(z + 3, 4)
    z_far = lax.rem(z + 2, 4)

    def device(s, h, b):
        return {"seq": s, "head": h, "batch": b}

    up = device(p * 8 + z_next * 2 + c, y, half)
    down = device(p * 8 + z_prev * 2 + c, y, half)
    flip = (1 - p) * 8 + z * 2 + c
    side = device(flip, y, half)
    other_side = device(flip, y, 1 - half)
    partner = device(p * 8 + z * 2 + 1 - c, y, half)
    y_up = device(seq, lax.rem(y + 1, 4), half)
    y_down = device(seq, lax.rem(y + 3, 4), half)
    later = device(lax.rem(seq + 1, 16), y, half)
    earlier = device(lax.rem(seq + 15, 16), y, half)
    quarter = lax.div(seq, 4)
    lane = lax.rem(seq, 4)
    moves = quarter != y
    perm_seq = 4 * y + lane
    perm = device(perm_seq, quarter, half)
    y_next = lax.rem(y + 1, 4)
    y_prev = lax.rem(y + 3, 4)

    def slab(r, q, zz, cc, part=None):
        if r < HEADS:
            ref = w_all.at[r, q, zz, cc]
            rows = 128
        else:
            ref = o_all.at[q, zz, cc]
            rows = 512
        if part is None:
            return ref
        return ref.at[pl.ds(part * (rows // 2), rows // 2)]

    def sent(src, dst, ss, rs, to):
        return pltpu.make_async_remote_copy(
            src_ref=src, dst_ref=dst, send_sem=ss, recv_sem=rs, device_id=to, device_id_type=MESH
        )

    def stage(h):
        cols = pl.ds(h * HEAD_DIM, HEAD_DIM)
        return [
            pltpu.make_async_copy(
                w.at[:, cols],
                w_all.at[h, p, z, c, :, pl.ds(n * HEAD_DIM, HEAD_DIM)],
                stage_sem.at[h, n],
            )
            for n, w in enumerate((w_query, w_key, w_value))
        ]

    token_copy = pltpu.make_async_copy(tokens, normed, load_sem.at[BLOCKS])
    bank_copies = [pltpu.make_async_copy(bank_hbm.at[b], bank.at[b], load_sem.at[b]) for b in range(BLOCKS)]
    perm_local = pltpu.make_async_copy(w_out, o_all.at[p, z, c], load_sem.at[BLOCKS + 1])
    perm_dst = o_all.at[lax.div(perm_seq, 8), lax.rem(lax.div(perm_seq, 2), 4), lax.rem(perm_seq, 2)]
    perm_copy = sent(w_out, perm_dst, perm_sem.at[0], perm_sem.at[1], perm)

    for copy in stage(0) + stage(1):
        copy.start()
    token_copy.start()
    for copy in stage(2) + stage(3):
        copy.start()
    for copy in bank_copies:
        copy.start()

    barrier = pltpu.get_barrier_semaphore()
    for peer in (up, down, side, other_side, partner, y_up, y_down, later, earlier):
        pl.semaphore_signal(barrier, inc=1, device_id=peer, device_id_type=MESH)

    @pl.when(moves)
    def _():
        pl.semaphore_signal(barrier, inc=1, device_id=perm, device_id_type=MESH)

    pl.semaphore_wait(barrier, 9 + moves.astype(jnp.int32))

    def w_copy(r, k):
        own = (p, z, c)
        before, after, far = (p, z_prev, c), (p, z_next, c), (p, z_far, c)
        where, part, to = {
            0: (own, None, up),
            1: (own, None, down),
            2: (before, 0, up),
            3: (after, 1, down),
            4: (own, 0, side),
            5: (own, 1, other_side),
            6: (before, 0, side),
            7: (before, 1, other_side),
            8: (after, 0, side),
            9: (after, 1, other_side),
            10: (far, 0, side),
            11: (far, 1, other_side),
            12: (own, None, partner),
            13: (before, None, partner),
            14: (after, None, partner),
            15: (far, None, partner),
        }[k]
        ref = slab(r, *where, part)
        return sent(ref, ref, w_send.at[r, k], w_recv.at[r, k], to)

    def w_far_side(r):
        ref = w_all.at[r, 1 - p, :, c] if r < HEADS else o_all.at[1 - p, :, c]
        return sent(ref, ref, w_send.at[r, 16], w_recv.at[r, 16], partner)

    def begin(r):
        if r < HEADS:
            for copy in stage(r):
                copy.wait()
        else:

            @pl.when(moves)
            def _():
                perm_copy.wait_recv()

            @pl.when(jnp.logical_not(moves))
            def _():
                perm_local.wait()

        for k in (0, 1, 4, 5, 12):
            w_copy(r, k).start()

    def relay(r):
        w_copy(r, 0).wait_recv()
        for k in (2, 6, 7, 13):
            w_copy(r, k).start()
        w_copy(r, 1).wait_recv()
        for k in (3, 8, 9, 14):
            w_copy(r, k).start()

    def relay_far(r):
        w_copy(r, 2).wait_recv()
        w_copy(r, 10).start()
        w_copy(r, 3).wait_recv()
        w_copy(r, 11).start()
        w_copy(r, 15).start()

    def cross(r):
        for k in range(4, 12):
            w_copy(r, k).wait_recv()
        w_far_side(r).start()

    def arrived(r):
        for k in range(12, 16):
            w_copy(r, k).wait_recv()
        w_far_side(r).wait_recv()

    def y_copy(h, g, k):
        n = h * GROUPS + g
        whose, part, to = {
            0: (y, None, y_up),
            1: (y, None, y_down),
            2: (y_prev, 0, y_up),
            3: (y_next, 1, y_down),
        }[k]
        if part is None:
            rows = pl.ds(g * GROUP_ROWS, GROUP_ROWS)
        else:
            rows = pl.ds(g * GROUP_ROWS + part * (GROUP_ROWS // 2), GROUP_ROWS // 2)
        ref = attended.at[h, whose, rows]
        return sent(ref, ref, y_send.at[n, k], y_recv.at[n, k], to)

    def share(n):
        for k in (0, 1):
            y_copy(n // GROUPS, n % GROUPS, k).start()

    def share_relay(n):
        h, g = n // GROUPS, n % GROUPS
        y_copy(h, g, 0).wait_recv()
        y_copy(h, g, 2).start()
        y_copy(h, g, 1).wait_recv()
        y_copy(h, g, 3).start()

    def share_done(n):
        for k in (2, 3):
            y_copy(n // GROUPS, n % GROUPS, k).wait_recv()

    def kv_hand(h):
        return sent(kv_send.at[h], kv_recv.at[h], kv_send_sem.at[h], kv_recv_sem.at[h], later)

    def normalize():
        def body(i, carry):
            rows = pl.ds(pl.multiple_of(i * 64, 64), 64)
            hidden = normed[rows, :].astype(F32)
            scale = lax.rsqrt(jnp.mean(hidden * hidden, axis=-1, keepdims=True) + 1e-06)
            normed[rows, :] = (hidden * scale).astype(BF16)
            return carry

        lax.fori_loop(0, ROWS // 64, body, 0)

    def weights(h, start, width):
        return w_all[h, :, :, :, :, pl.ds(start, width)].reshape(D, width)

    def project_queries(h):
        def body(i, carry):
            rows = pl.ds(pl.multiple_of(i * 256, 256), 256)
            queries[h % 2, rows, :] = jnp.dot(
                normed[rows, :], weights(h, 0, HEAD_DIM), preferred_element_type=F32
            ).astype(BF16)
            return carry

        lax.fori_loop(0, ROWS // 256, body, 0)

    def project_pair(h, first, second):
        rows = jnp.concatenate([bank[slots[first]], bank[slots[second]]], axis=0)
        return jnp.dot(rows, weights(h, HEAD_DIM, 2 * HEAD_DIM), preferred_element_type=F32).astype(BF16)

    def attend(h, position, keys, values, first=False):
        block = 0 if first else position + 1
        row = block * BLOCK
        if not isinstance(row, int):
            row = pl.multiple_of(row, BLOCK)
        q = queries[h % 2, pl.ds(row, BLOCK), :]
        scores = lax.dot_general(q, keys, (((1,), (1,)), ((), ())), preferred_element_type=F32) * SCALE
        peak = jnp.max(scores, axis=-1, keepdims=True)
        exponent = jnp.exp(scores - peak)
        inverse = 1.0 / jnp.sum(exponent, axis=-1, keepdims=True)
        probs = (exponent * inverse).astype(BF16)
        mixed = jnp.dot(probs, values, preferred_element_type=F32)
        if first:
            mixed = jnp.where(seq == 0, jnp.zeros_like(mixed), mixed)
        at = position * BLOCK
        if not isinstance(at, int):
            at = pl.multiple_of(at, BLOCK)
        attended[h, y, pl.ds(at, BLOCK), :] = mixed.astype(BF16)

    def from_pair(parity, which):
        rows = pl.ds(which * KEYS, KEYS)
        return kv_pairs[parity, rows, 0:HEAD_DIM], kv_pairs[parity, rows, HEAD_DIM : 2 * HEAD_DIM]

    def from_earlier(h):
        return kv_recv[h, :, 0:HEAD_DIM], kv_recv[h, :, HEAD_DIM : 2 * HEAD_DIM]

    def step(h, i, parity):
        if isinstance(i, int) and i == 0:
            if h > 0:
                attend(h - 1, 13, *from_pair(1, 0))
                attend(h - 1, 14, *from_pair(1, 1))
            pair = project_pair(h, 15, 0)
            kv_send[h] = pair[0:KEYS]
            kv_pairs[0, KEYS : 2 * KEYS, :] = pair[KEYS : 2 * KEYS]
            return
        if isinstance(i, int) and i == 1:
            if h > 0:
                kv_hand(h - 1).wait_recv()
                attend(h - 1, 15, *from_earlier(h - 1), first=True)
            attend(h, 0, *from_pair(0, 1))
        else:
            attend(h, 2 * i - 3, *from_pair(1 - parity, 0))
            attend(h, 2 * i - 2, *from_pair(1 - parity, 1))
        kv_pairs[parity] = project_pair(h, 2 * i - 1, 2 * i)

    def out_weights(h):
        rows = pl.ds(h * 128, 128)
        return jnp.concatenate(
            [
                jnp.concatenate([o_all[t // 8, (t // 2) % 4, t % 2, rows, :] for t in range(4 * g, 4 * g + 4)], axis=1)
                for g in range(4)
            ],
            axis=0,
        )

    def project_out(n):
        h, g = n // GROUPS, n % GROUPS
        rows = pl.ds(g * GROUP_ROWS, GROUP_ROWS)
        wide = jnp.concatenate([attended[h, g2, rows, :] for g2 in range(4)], axis=1)
        added = jnp.dot(wide, out_weights(h), preferred_element_type=F32)
        if h == 0:
            total[rows, :] = added
        elif h < HEADS - 1:
            total[rows, :] += added
        else:
            done = (total[rows, :] + added).astype(BF16)
            start = g * GROUP_ROWS + BLOCK
            if g < GROUPS - 1:
                out[start : start + GROUP_ROWS, :] = done
            else:
                out[start:ROWS, :] = done[: GROUP_ROWS - BLOCK]
                out[0:BLOCK, :] = done[GROUP_ROWS - BLOCK :]

    begin(0)

    @pl.when(moves)
    def _():
        perm_copy.start()

    @pl.when(jnp.logical_not(moves))
    def _():
        perm_local.start()

    begin(1)
    token_copy.wait()
    normalize()
    relay(0)
    relay_far(0)
    relay(1)
    cross(0)
    for copy in bank_copies:
        copy.wait()
    arrived(0)

    after = {
        (0, 0): [lambda: relay_far(1), lambda: begin(2)],
        (0, 3): [lambda: cross(1), lambda: relay(2)],
        (0, 5): [lambda: relay_far(2), lambda: begin(3), lambda: share(0)],
        (0, 7): [lambda: cross(2), lambda: arrived(1)],
        (1, 0): [lambda: relay(3)],
        (1, 1): [lambda: relay_far(3), lambda: begin(4), lambda: share(1)],
        (1, 3): [lambda: cross(3), lambda: relay(4)],
        (1, 5): [lambda: relay_far(4), lambda: share_relay(0), lambda: share(2)],
        (1, 7): [lambda: arrived(2)],
        (2, 1): [lambda: share(3), lambda: share_relay(1), lambda: cross(4)],
        (2, 5): [lambda: share_relay(2), lambda: share(4)],
        (2, 7): [lambda: arrived(3)],
        (3, 1): [lambda: share(5), lambda: share_relay(3), lambda: arrived(4)],
        (3, 5): [lambda: share(6)],
        (3, 7): [lambda: share_relay(4)],
    }

    def ticks(h, i):
        for f in after.get((h, i), ()):
            f()

    for h in range(HEADS):
        project_queries(h)
        step(h, 0, 0)
        ticks(h, 0)
        step(h, 1, 1)
        kv_hand(h).start()
        ticks(h, 1)
        for stretch in ((2, 4), (4, 6), (6, 8)):
            step(h, stretch[0], 0)
            step(h, stretch[0] + 1, 1)
            ticks(h, stretch[1] - 1)

    last = HEADS - 1
    attend(last, 13, *from_pair(1, 0))
    attend(last, 14, *from_pair(1, 1))
    kv_hand(last).wait_recv()
    attend(last, 15, *from_earlier(last), first=True)
    share_done(0)
    project_out(0)
    share(7)
    share_done(1)
    project_out(1)
    share_relay(5)
    share_done(2)
    project_out(2)
    share_done(3)
    project_out(3)
    share_relay(6)
    share_done(4)
    project_out(4)
    share_relay(7)
    share_done(5)
    project_out(5)
    share_done(6)
    project_out(6)
    share_done(7)
    project_out(7)

    for r in range(HEADS + 1):
        for k in range(16):
            w_copy(r, k).wait_send()
        w_far_side(r).wait_send()
    for n in range(HEADS * GROUPS):
        for k in range(4):
            y_copy(n // GROUPS, n % GROUPS, k).wait_send()
    for h in range(HEADS):
        kv_hand(h).wait_send()

    @pl.when(moves)
    def _():
        perm_copy.wait_send()


def local(tokens, neighbor_bank, slots, w_query, w_key, w_value, w_out):
    hbm = pl.BlockSpec(memory_space=pl.ANY)
    return pl.pallas_call(
        kernel,
        out_shape=jax.ShapeDtypeStruct((ROWS, HEADS * HEAD_DIM), BF16),
        in_specs=[hbm, hbm, pl.BlockSpec(memory_space=pltpu.SMEM), hbm, hbm, hbm, hbm],
        out_specs=pl.BlockSpec(memory_space=pltpu.VMEM),
        scratch_shapes=[
            pltpu.VMEM((ROWS, D), BF16),
            pltpu.VMEM((BLOCKS, KEYS, D), BF16),
            pltpu.VMEM((HEADS, 2, 4, 2, 128, 3 * HEAD_DIM), BF16),
            pltpu.VMEM((2, 4, 2, 512, 128), BF16),
            pltpu.VMEM((2, ROWS, HEAD_DIM), BF16),
            pltpu.VMEM((2, 2 * KEYS, 2 * HEAD_DIM), BF16),
            pltpu.VMEM((HEADS, KEYS, 2 * HEAD_DIM), BF16),
            pltpu.VMEM((HEADS, KEYS, 2 * HEAD_DIM), BF16),
            pltpu.VMEM((HEADS, 4, ROWS, HEAD_DIM), BF16),
            pltpu.VMEM((ROWS, 512), F32),
            pltpu.SemaphoreType.DMA((HEADS, 3)),
            pltpu.SemaphoreType.DMA((BLOCKS + 2,)),
            pltpu.SemaphoreType.DMA((HEADS + 1, 17)),
            pltpu.SemaphoreType.DMA((HEADS + 1, 17)),
            pltpu.SemaphoreType.DMA((HEADS * GROUPS, 4)),
            pltpu.SemaphoreType.DMA((HEADS * GROUPS, 4)),
            pltpu.SemaphoreType.DMA((HEADS,)),
            pltpu.SemaphoreType.DMA((HEADS,)),
            pltpu.SemaphoreType.DMA((2,)),
        ],
        compiler_params=pltpu.CompilerParams(
            collective_id=0, has_side_effects=True, vmem_limit_bytes=64 * 1024 * 1024 - 512 * 1024
        ),
        name="attention",
    )(tokens, neighbor_bank, slots, w_query, w_key, w_value, w_out)


def solution(mesh):
    in_specs = (
        P(("batch", "seq"), None),
        P(("batch", "seq"), None, None),
        P(("batch", "seq")),
        P("seq", "head"),
        P("seq", "head"),
        P("seq", "head"),
        P("head", "seq"),
    )
    out_specs = P(("batch", "seq"), "head")
    return jax.shard_map(local, mesh=mesh, in_specs=in_specs, out_specs=out_specs, check_vma=False)
```

time: 215 us -> 112 us (0.52)
  the two profiles are of different devices: /device:TPU:3 before, /device:TPU:0 now
where the time goes in v1:
time: 112 us
  Pallas kernels  110 us (98%)
  local copies, waits for them, and re-layouts  2.26 us (2%)
    pallas_call x1, Pallas kernels, local(): pl.pallas_call(kernel, out_shape=jax.ShapeDtypeStruct((ROWS, HEADS * HEAD...  110 us
    unnamed x1, local copies, waits for them, and re-layouts  2.26 us

profile of v1, /device:TPU:0, one launch (start us, length us, event | category | flops | bytes accessed | tf_op | source)
XLA Modules:
  0.0 111.9 jit_solution(9154067181259723380)
XLA Ops:
  0.0 109.6 %attention.1 = bf16[1024,512]{1,0:T(8,128)(2,1)} custom-call(bf16[1024,2048]{1,0:T(8,128)(2,1)} %tokens.1, bf16[16,256,2048]{2,1,0:T(8,128)(2,1)} %bank_hbm.1, s32[16]{0:T(128)} %slots.1, bf16[128,512]{1,0:T(8,128)(2,1)} %w_query.1, bf16[128,512]{1,0:T(8,128)(2,1)} %w_key.1, bf16[128,512]{1,0:T(8,128)(2,1)} %w_value.1, bf16[512,128]{1,0:T(8,128)(2,1)} %w_out.1), custom_call_target="tpu_custom_call" | custom-call | tf_op jit(solution)/shard_map/attention/pallas_call | solution.py:438
  109.6 2.3 %copy.9 = bf16[1024,512]{1,0:T(8,128)(2,1)} copy(bf16[1024,512]{1,0:T(8,128)(2,1)} %attention.1) | data formatting | bytes 2097152

commit v2 on v1

--- a/solution.py
+++ b/solution.py
@@ -18,6 +18,12 @@
 HEADS = 4
 GROUPS = 2
 GROUP_ROWS = ROWS // GROUPS
+WIDTH = 2 * HEAD_DIM
+KV_ROUND = (0, 2, 3, 5)
+Q_ROUND = (1, 4)
+O_ROUND = 6
+KV_IN = 2 * BLOCKS
+KV_OUT = KV_IN + HEADS + 1
 SCALE = 1.0 / math.sqrt(HEAD_DIM)
 BF16 = jnp.bfloat16
 F32 = jnp.float32
@@ -37,9 +43,7 @@
     w_all,
     o_all,
     queries,
-    kv_pairs,
-    kv_send,
-    kv_recv,
+    kv,
     attended,
     total,
     stage_sem,
@@ -84,7 +88,7 @@
     y_prev = lax.rem(y + 3, 4)
 
     def slab(r, q, zz, cc, part=None):
-        if r < HEADS:
+        if r < O_ROUND:
             ref = w_all.at[r, q, zz, cc]
             rows = 128
         else:
@@ -99,15 +103,17 @@
             src_ref=src, dst_ref=dst, send_sem=ss, recv_sem=rs, device_id=to, device_id_type=MESH
         )
 
-    def stage(h):
-        cols = pl.ds(h * HEAD_DIM, HEAD_DIM)
+    def stage(r):
+        if r in Q_ROUND:
+            parts = [(w_query, Q_ROUND.index(r) * WIDTH, 0, WIDTH)]
+        else:
+            h = KV_ROUND.index(r)
+            parts = [(w_key, h * HEAD_DIM, 0, HEAD_DIM), (w_value, h * HEAD_DIM, HEAD_DIM, HEAD_DIM)]
         return [
             pltpu.make_async_copy(
-                w.at[:, cols],
-                w_all.at[h, p, z, c, :, pl.ds(n * HEAD_DIM, HEAD_DIM)],
-                stage_sem.at[h, n],
+                w.at[:, pl.ds(start, width)], w_all.at[r, p, z, c, :, pl.ds(at, width)], stage_sem.at[r, n]
             )
-            for n, w in enumerate((w_query, w_key, w_value))
+            for n, (w, start, at, width) in enumerate(parts)
         ]
 
     token_copy = pltpu.make_async_copy(tokens, normed, load_sem.at[BLOCKS])
@@ -116,14 +122,6 @@
     perm_dst = o_all.at[lax.div(perm_seq, 8), lax.rem(lax.div(perm_seq, 2), 4), lax.rem(perm_seq, 2)]
     perm_copy = sent(w_out, perm_dst, perm_sem.at[0], perm_sem.at[1], perm)
 
-    for copy in stage(0) + stage(1):
-        copy.start()
-    token_copy.start()
-    for copy in stage(2) + stage(3):
-        copy.start()
-    for copy in bank_copies:
-        copy.start()
-
     barrier = pltpu.get_barrier_semaphore()
     for peer in (up, down, side, other_side, partner, y_up, y_down, later, earlier):
         pl.semaphore_signal(barrier, inc=1, device_id=peer, device_id_type=MESH)
@@ -131,6 +129,12 @@
     @pl.when(moves)
     def _():
         pl.semaphore_signal(barrier, inc=1, device_id=perm, device_id_type=MESH)
+
+    for r in range(O_ROUND):
+        for copy in stage(r):
+            copy.start()
+        if r == 1:
+            token_copy.start()
 
     pl.semaphore_wait(barrier, 9 + moves.astype(jnp.int32))
 
@@ -159,11 +163,11 @@
         return sent(ref, ref, w_send.at[r, k], w_recv.at[r, k], to)
 
     def w_far_side(r):
-        ref = w_all.at[r, 1 - p, :, c] if r < HEADS else o_all.at[1 - p, :, c]
+        ref = w_all.at[r, 1 - p, :, c] if r < O_ROUND else o_all.at[1 - p, :, c]
         return sent(ref, ref, w_send.at[r, 16], w_recv.at[r, 16], partner)
 
     def begin(r):
-        if r < HEADS:
+        if r < O_ROUND:
             for copy in stage(r):
                 copy.wait()
         else:
@@ -216,7 +220,7 @@
             rows = pl.ds(g * GROUP_ROWS, GROUP_ROWS)
         else:
             rows = pl.ds(g * GROUP_ROWS + part * (GROUP_ROWS // 2), GROUP_ROWS // 2)
-        ref = attended.at[h, whose, rows]
+        ref = attended.at[h + 1, whose, rows]
         return sent(ref, ref, y_send.at[n, k], y_recv.at[n, k], to)
 
     def share(n):
@@ -235,7 +239,7 @@
             y_copy(n // GROUPS, n % GROUPS, k).wait_recv()
 
     def kv_hand(h):
-        return sent(kv_send.at[h], kv_recv.at[h], kv_send_sem.at[h], kv_recv_sem.at[h], later)
+        return sent(kv.at[KV_OUT + h], kv.at[KV_IN + h + 1], kv_send_sem.at[h], kv_recv_sem.at[h], later)
 
     def normalize():
         def body(i, carry):
@@ -247,67 +251,69 @@
 
         lax.fori_loop(0, ROWS // 64, body, 0)
 
-    def weights(h, start, width):
-        return w_all[h, :, :, :, :, pl.ds(start, width)].reshape(D, width)
-
-    def project_queries(h):
-        def body(i, carry):
-            rows = pl.ds(pl.multiple_of(i * 256, 256), 256)
-            queries[h % 2, rows, :] = jnp.dot(
-                normed[rows, :], weights(h, 0, HEAD_DIM), preferred_element_type=F32
-            ).astype(BF16)
-            return carry
-
-        lax.fori_loop(0, ROWS // 256, body, 0)
-
-    def project_pair(h, first, second):
-        rows = jnp.concatenate([bank[slots[first]], bank[slots[second]]], axis=0)
-        return jnp.dot(rows, weights(h, HEAD_DIM, 2 * HEAD_DIM), preferred_element_type=F32).astype(BF16)
-
-    def attend(h, position, keys, values, first=False):
-        block = 0 if first else position + 1
-        row = block * BLOCK
-        if not isinstance(row, int):
-            row = pl.multiple_of(row, BLOCK)
-        q = queries[h % 2, pl.ds(row, BLOCK), :]
-        scores = lax.dot_general(q, keys, (((1,), (1,)), ((), ())), preferred_element_type=F32) * SCALE
-        peak = jnp.max(scores, axis=-1, keepdims=True)
-        exponent = jnp.exp(scores - peak)
+    def weights(r):
+        return w_all[r].reshape(D, WIDTH)
+
+    def project_queries(pair):
+        both = jnp.dot(normed[...], weights(1 + 3 * pair), preferred_element_type=F32).astype(BF16)
+        queries[2 * pair + 1] = both[:, 0:HEAD_DIM]
+        queries[2 * pair + 2] = both[:, HEAD_DIM:WIDTH]
+
+    def place(task):
+        return lax.div(task, BLOCKS), lax.rem(task, BLOCKS)
+
+    def scores_of(tasks):
+        scores, values = [], []
+        for task in tasks:
+            slot, position = place(task)
+            handed = lax.div(position, BLOCKS - 1)
+            rows = kv[handed * (KV_IN + slot) + (1 - handed) * (lax.rem(slot, 2) * BLOCKS + position)]
+            block = lax.rem(position + 1, BLOCKS)
+            q = queries[slot, pl.ds(pl.multiple_of(block * BLOCK, BLOCK), BLOCK), :]
+            scores.append(
+                lax.dot_general(q, rows[:, 0:HEAD_DIM], (((1,), (1,)), ((), ())), preferred_element_type=F32) * SCALE
+            )
+            values.append(rows[:, HEAD_DIM:WIDTH])
+        return scores, values
+
+    def probs_of(scores):
+        joined = jnp.concatenate(scores, axis=0)
+        exponent = jnp.exp(joined - jnp.max(joined, axis=-1, keepdims=True))
         inverse = 1.0 / jnp.sum(exponent, axis=-1, keepdims=True)
         probs = (exponent * inverse).astype(BF16)
-        mixed = jnp.dot(probs, values, preferred_element_type=F32)
-        if first:
-            mixed = jnp.where(seq == 0, jnp.zeros_like(mixed), mixed)
-        at = position * BLOCK
-        if not isinstance(at, int):
-            at = pl.multiple_of(at, BLOCK)
-        attended[h, y, pl.ds(at, BLOCK), :] = mixed.astype(BF16)
-
-    def from_pair(parity, which):
-        rows = pl.ds(which * KEYS, KEYS)
-        return kv_pairs[parity, rows, 0:HEAD_DIM], kv_pairs[parity, rows, HEAD_DIM : 2 * HEAD_DIM]
-
-    def from_earlier(h):
-        return kv_recv[h, :, 0:HEAD_DIM], kv_recv[h, :, HEAD_DIM : 2 * HEAD_DIM]
-
-    def step(h, i, parity):
-        if isinstance(i, int) and i == 0:
-            if h > 0:
-                attend(h - 1, 13, *from_pair(1, 0))
-                attend(h - 1, 14, *from_pair(1, 1))
-            pair = project_pair(h, 15, 0)
-            kv_send[h] = pair[0:KEYS]
-            kv_pairs[0, KEYS : 2 * KEYS, :] = pair[KEYS : 2 * KEYS]
-            return
-        if isinstance(i, int) and i == 1:
-            if h > 0:
-                kv_hand(h - 1).wait_recv()
-                attend(h - 1, 15, *from_earlier(h - 1), first=True)
-            attend(h, 0, *from_pair(0, 1))
-        else:
-            attend(h, 2 * i - 3, *from_pair(1 - parity, 0))
-            attend(h, 2 * i - 2, *from_pair(1 - parity, 1))
-        kv_pairs[parity] = project_pair(h, 2 * i - 1, 2 * i)
+        return [probs[n * BLOCK : (n + 1) * BLOCK] for n in range(len(scores))]
+
+    def mix(tasks, probs, values):
+        mixed = []
+        for task, weight, rows in zip(tasks, probs, values):
+            one = jnp.dot(weight, rows, preferred_element_type=F32)
+            empty = jnp.logical_and(lax.rem(task, BLOCKS) == BLOCKS - 1, seq == 0)
+            mixed.append(jnp.where(empty, jnp.zeros_like(one), one).astype(BF16))
+        return mixed
+
+    def keep(tasks, mixed):
+        for task, rows in zip(tasks, mixed):
+            slot, position = place(task)
+            attended[slot, y, pl.ds(pl.multiple_of(position * BLOCK, BLOCK), BLOCK), :] = rows
+
+    def attend(tasks):
+        scores, values = scores_of(tasks)
+        keep(tasks, mix(tasks, probs_of(scores), values))
+
+    def step(h, i):
+        n = 8 * h + i
+        tasks = [2 * n + 13, 2 * n + 14]
+        scores, values = scores_of(tasks)
+        probs = probs_of(scores)
+        first, second = lax.rem(2 * i + 15, BLOCKS), 2 * i
+        rows = jnp.concatenate([bank[slots[first]], bank[slots[second]]], axis=0)
+        pair = jnp.dot(rows, weights(h + lax.div(h + 1, 2)), preferred_element_type=F32).astype(BF16)
+        mixed = mix(tasks, probs, values)
+        own = lax.rem(h + 1, 2) * BLOCKS
+        later_step = lax.div(i + 7, 8)
+        kv[(1 - later_step) * (KV_OUT + h) + later_step * (own + first)] = pair[0:KEYS]
+        kv[own + second] = pair[KEYS : 2 * KEYS]
+        keep(tasks, mixed)
 
     def out_weights(h):
         rows = pl.ds(h * 128, 128)
@@ -322,7 +328,7 @@
     def project_out(n):
         h, g = n // GROUPS, n % GROUPS
         rows = pl.ds(g * GROUP_ROWS, GROUP_ROWS)
-        wide = jnp.concatenate([attended[h, g2, rows, :] for g2 in range(4)], axis=1)
+        wide = jnp.concatenate([attended[h + 1, g2, rows, :] for g2 in range(4)], axis=1)
         added = jnp.dot(wide, out_weights(h), preferred_element_type=F32)
         if h == 0:
             total[rows, :] = added
@@ -337,20 +343,28 @@
                 out[start:ROWS, :] = done[: GROUP_ROWS - BLOCK]
                 out[0:BLOCK, :] = done[GROUP_ROWS - BLOCK :]
 
+    def swap_out_weights():
+        @pl.when(moves)
+        def _():
+            perm_copy.start()
+
+        @pl.when(jnp.logical_not(moves))
+        def _():
+            perm_local.start()
+
+    def load_bank():
+        for copy in bank_copies:
+            copy.start()
+
+    def catch_up():
+        attend([BLOCKS + n for n in range(7)])
+
     begin(0)
-
-    @pl.when(moves)
-    def _():
-        perm_copy.start()
-
-    @pl.when(jnp.logical_not(moves))
-    def _():
-        perm_local.start()
-
-    begin(1)
     token_copy.wait()
     normalize()
     relay(0)
+    load_bank()
+    begin(1)
     relay_far(0)
     relay(1)
     cross(0)
@@ -359,44 +373,64 @@
     arrived(0)
 
     after = {
-        (0, 0): [lambda: relay_far(1), lambda: begin(2)],
-        (0, 3): [lambda: cross(1), lambda: relay(2)],
-        (0, 5): [lambda: relay_far(2), lambda: begin(3), lambda: share(0)],
-        (0, 7): [lambda: cross(2), lambda: arrived(1)],
-        (1, 0): [lambda: relay(3)],
-        (1, 1): [lambda: relay_far(3), lambda: begin(4), lambda: share(1)],
-        (1, 3): [lambda: cross(3), lambda: relay(4)],
-        (1, 5): [lambda: relay_far(4), lambda: share_relay(0), lambda: share(2)],
-        (1, 7): [lambda: arrived(2)],
-        (2, 1): [lambda: share(3), lambda: share_relay(1), lambda: cross(4)],
-        (2, 5): [lambda: share_relay(2), lambda: share(4)],
-        (2, 7): [lambda: arrived(3)],
-        (3, 1): [lambda: share(5), lambda: share_relay(3), lambda: arrived(4)],
-        (3, 5): [lambda: share(6)],
-        (3, 7): [lambda: share_relay(4)],
+        (0, 0): [(relay_far, 1), (begin, 2)],
+        (0, 1): [(swap_out_weights,)],
+        (0, 2): [(relay, 2)],
+        (0, 3): [(cross, 1)],
+        (0, 4): [(arrived, 1), (project_queries, 0), (catch_up,), (relay_far, 2), (begin, 3)],
+        (0, 5): [(share, 0)],
+        (0, 6): [(cross, 2), (relay, 3)],
+        (0, 7): [(arrived, 2), (begin, 4)],
+        (1, 0): [(relay_far, 3)],
+        (1, 1): [(relay, 4), (begin, 5), (share, 1)],
+        (1, 2): [(cross, 3)],
+        (1, 3): [(relay_far, 4), (share_relay, 0)],
+        (1, 4): [(relay, 5), (cross, 4), (begin, 6)],
+        (1, 5): [(share, 2)],
+        (1, 6): [(relay_far, 5)],
+        (1, 7): [(arrived, 3), (arrived, 4), (share_relay, 1), (project_queries, 1)],
+        (2, 0): [(cross, 5), (relay, 6)],
+        (2, 1): [(share, 3)],
+        (2, 2): [(relay_far, 6)],
+        (2, 3): [(arrived, 5), (share_relay, 2)],
+        (2, 4): [(cross, 6)],
+        (2, 5): [(share, 4)],
+        (2, 7): [(share_relay, 3)],
+        (3, 1): [(share, 5)],
+        (3, 5): [(share_relay, 4), (share, 6)],
+        (3, 7): [(arrived, 6)],
     }
 
-    def ticks(h, i):
-        for f in after.get((h, i), ()):
-            f()
-
-    for h in range(HEADS):
-        project_queries(h)
-        step(h, 0, 0)
-        ticks(h, 0)
-        step(h, 1, 1)
-        kv_hand(h).start()
-        ticks(h, 1)
-        for stretch in ((2, 4), (4, 6), (6, 8)):
-            step(h, stretch[0], 0)
-            step(h, stretch[0] + 1, 1)
-            ticks(h, stretch[1] - 1)
-
-    last = HEADS - 1
-    attend(last, 13, *from_pair(1, 0))
-    attend(last, 14, *from_pair(1, 1))
-    kv_hand(last).wait_recv()
-    attend(last, 15, *from_earlier(last), first=True)
+    def one_step(n, carry):
+        h, i = lax.div(n, 8), lax.rem(n, 8)
+        step(h, i)
+
+        @pl.when(i == 1)
+        def _():
+            kv_hand(h).start()
+
+        @pl.when(jnp.logical_and(i == 0, h > 0))
+        def _():
+            kv_hand(h - 1).wait_recv()
+
+        for head in range(HEADS):
+
+            @pl.when(h == head)
+            def _(head=head):
+                for (at, place_in), actions in after.items():
+                    if at == head:
+
+                        @pl.when(i == place_in)
+                        def _(actions=actions):
+                            for action, *rest in actions:
+                                action(*rest)
+
+        return carry
+
+    lax.fori_loop(0, 8 * HEADS, one_step, 0)
+
+    kv_hand(HEADS - 1).wait_recv()
+    attend([BLOCKS * HEADS + n for n in (13, 14, 15)])
     share_done(0)
     project_out(0)
     share(7)
@@ -418,7 +452,7 @@
     share_done(7)
     project_out(7)
 
-    for r in range(HEADS + 1):
+    for r in range(O_ROUND + 1):
         for k in range(16):
             w_copy(r, k).wait_send()
         w_far_side(r).wait_send()
@@ -443,18 +477,16 @@
         scratch_shapes=[
             pltpu.VMEM((ROWS, D), BF16),
             pltpu.VMEM((BLOCKS, KEYS, D), BF16),
-            pltpu.VMEM((HEADS, 2, 4, 2, 128, 3 * HEAD_DIM), BF16),
+            pltpu.VMEM((O_ROUND, 2, 4, 2, 128, WIDTH), BF16),
             pltpu.VMEM((2, 4, 2, 512, 128), BF16),
-            pltpu.VMEM((2, ROWS, HEAD_DIM), BF16),
-            pltpu.VMEM((2, 2 * KEYS, 2 * HEAD_DIM), BF16),
-            pltpu.VMEM((HEADS, KEYS, 2 * HEAD_DIM), BF16),
-            pltpu.VMEM((HEADS, KEYS, 2 * HEAD_DIM), BF16),
-            pltpu.VMEM((HEADS, 4, ROWS, HEAD_DIM), BF16),
+            pltpu.VMEM((HEADS + 1, ROWS, HEAD_DIM), BF16),
+            pltpu.VMEM((KV_OUT + HEADS, KEYS, WIDTH), BF16),
+            pltpu.VMEM((HEADS + 1, 4, ROWS, HEAD_DIM), BF16),
             pltpu.VMEM((ROWS, 512), F32),
-            pltpu.SemaphoreType.DMA((HEADS, 3)),
+            pltpu.SemaphoreType.DMA((O_ROUND, 2)),
             pltpu.SemaphoreType.DMA((BLOCKS + 2,)),
-            pltpu.SemaphoreType.DMA((HEADS + 1, 17)),
-            pltpu.SemaphoreType.DMA((HEADS + 1, 17)),
+            pltpu.SemaphoreType.DMA((O_ROUND + 1, 17)),
+            pltpu.SemaphoreType.DMA((O_ROUND + 1, 17)),
             pltpu.SemaphoreType.DMA((HEADS * GROUPS, 4)),
             pltpu.SemaphoreType.DMA((HEADS * GROUPS, 4)),
             pltpu.SemaphoreType.DMA((HEADS,)),

time: 112 us -> 89.9 us (0.80)
  Pallas kernels: 110 us -> 87.1 us
    pallas_call x1, Pallas kernels: 110 us -> 87.1 us  [local(): pl.pallas_call(kernel, out_shape=jax.ShapeDtypeStruct((ROWS, HEADS * HEAD...]
where the time goes in v2:
time: 89.9 us; the launch traced here: 89.3 us
  Pallas kernels  87.1 us (97%)
  local copies, waits for them, and re-layouts  2.26 us (3%)
    pallas_call x1, Pallas kernels, local(): pl.pallas_call(kernel, out_shape=jax.ShapeDtypeStruct((ROWS, HEADS * HEAD...  87.1 us
    unnamed x1, local copies, waits for them, and re-layouts  2.26 us

profile of v2, /device:TPU:0, one launch (start us, length us, event | category | flops | bytes accessed | tf_op | source)
XLA Modules:
  0.0 89.3 jit_solution(7265606558133216901)
XLA Ops:
  0.0 87.1 %attention.1 = bf16[1024,512]{1,0:T(8,128)(2,1)} custom-call(bf16[1024,2048]{1,0:T(8,128)(2,1)} %tokens.1, bf16[16,256,2048]{2,1,0:T(8,128)(2,1)} %bank_hbm.1, s32[16]{0:T(128)} %slots.1, bf16[128,512]{1,0:T(8,128)(2,1)} %w_query.1, bf16[128,512]{1,0:T(8,128)(2,1)} %w_key.1, bf16[128,512]{1,0:T(8,128)(2,1)} %w_value.1, bf16[512,128]{1,0:T(8,128)(2,1)} %w_out.1), custom_call_target="tpu_custom_call" | custom-call | tf_op jit(solution)/shard_map/attention/pallas_call | solution.py:472
  87.1 2.3 %copy.9 = bf16[1024,512]{1,0:T(8,128)(2,1)} copy(bf16[1024,512]{1,0:T(8,128)(2,1)} %attention.1) | data formatting | bytes 2097152

commit v3 on v2

--- a/solution.py
+++ b/solution.py
@@ -16,8 +16,18 @@
 D = 2048
 ROWS = BLOCKS * BLOCK
 HEADS = 4
-GROUPS = 2
-GROUP_ROWS = ROWS // GROUPS
+PIECES = (
+    (0, 0, 256),
+    (0, 256, 256),
+    (0, 512, 512),
+    (1, 0, 512),
+    (1, 512, 512),
+    (2, 0, 512),
+    (2, 512, 512),
+    (3, 0, 512),
+    (3, 512, 256),
+    (3, 768, 256),
+)
 WIDTH = 2 * HEAD_DIM
 KV_ROUND = (0, 2, 3, 5)
 Q_ROUND = (1, 4)
@@ -75,6 +85,12 @@
     side = device(flip, y, half)
     other_side = device(flip, y, 1 - half)
     partner = device(p * 8 + z * 2 + 1 - c, y, half)
+    cross_up = (1 - p) * 8 + z_next * 2 + c
+    cross_down = (1 - p) * 8 + z_prev * 2 + c
+    side_up = device(cross_up, y, half)
+    side_down = device(cross_down, y, half)
+    other_up = device(cross_up, y, 1 - half)
+    other_down = device(cross_down, y, 1 - half)
     y_up = device(seq, lax.rem(y + 1, 4), half)
     y_down = device(seq, lax.rem(y + 3, 4), half)
     later = device(lax.rem(seq + 1, 16), y, half)
@@ -123,7 +139,8 @@
     perm_copy = sent(w_out, perm_dst, perm_sem.at[0], perm_sem.at[1], perm)
 
     barrier = pltpu.get_barrier_semaphore()
-    for peer in (up, down, side, other_side, partner, y_up, y_down, later, earlier):
+    near = (up, down, side, other_side, partner, side_up, side_down, other_up, other_down)
+    for peer in near + (y_up, y_down, later, earlier):
         pl.semaphore_signal(barrier, inc=1, device_id=peer, device_id_type=MESH)
 
     @pl.when(moves)
@@ -136,7 +153,7 @@
         if r == 1:
             token_copy.start()
 
-    pl.semaphore_wait(barrier, 9 + moves.astype(jnp.int32))
+    pl.semaphore_wait(barrier, 13 + moves.astype(jnp.int32))
 
     def w_copy(r, k):
         own = (p, z, c)
@@ -152,8 +169,8 @@
             7: (before, 1, other_side),
             8: (after, 0, side),
             9: (after, 1, other_side),
-            10: (far, 0, side),
-            11: (far, 1, other_side),
+            10: (before, 0, side_up),
+            11: (after, 1, other_down),
             12: (own, None, partner),
             13: (before, None, partner),
             14: (after, None, partner),
@@ -185,17 +202,15 @@
 
     def relay(r):
         w_copy(r, 0).wait_recv()
-        for k in (2, 6, 7, 13):
+        for k in (2, 10, 6, 7, 13):
             w_copy(r, k).start()
         w_copy(r, 1).wait_recv()
-        for k in (3, 8, 9, 14):
+        for k in (3, 11, 8, 9, 14):
             w_copy(r, k).start()
 
     def relay_far(r):
         w_copy(r, 2).wait_recv()
-        w_copy(r, 10).start()
         w_copy(r, 3).wait_recv()
-        w_copy(r, 11).start()
         w_copy(r, 15).start()
 
     def cross(r):
@@ -208,35 +223,31 @@
             w_copy(r, k).wait_recv()
         w_far_side(r).wait_recv()
 
-    def y_copy(h, g, k):
-        n = h * GROUPS + g
+    def y_copy(n, k):
+        h, start, count = PIECES[n]
         whose, part, to = {
             0: (y, None, y_up),
             1: (y, None, y_down),
             2: (y_prev, 0, y_up),
             3: (y_next, 1, y_down),
         }[k]
-        if part is None:
-            rows = pl.ds(g * GROUP_ROWS, GROUP_ROWS)
-        else:
-            rows = pl.ds(g * GROUP_ROWS + part * (GROUP_ROWS // 2), GROUP_ROWS // 2)
+        rows = pl.ds(start, count) if part is None else pl.ds(start + part * (count // 2), count // 2)
         ref = attended.at[h + 1, whose, rows]
         return sent(ref, ref, y_send.at[n, k], y_recv.at[n, k], to)
 
     def share(n):
         for k in (0, 1):
-            y_copy(n // GROUPS, n % GROUPS, k).start()
+            y_copy(n, k).start()
 
     def share_relay(n):
-        h, g = n // GROUPS, n % GROUPS
-        y_copy(h, g, 0).wait_recv()
-        y_copy(h, g, 2).start()
-        y_copy(h, g, 1).wait_recv()
-        y_copy(h, g, 3).start()
+        y_copy(n, 0).wait_recv()
+        y_copy(n, 2).start()
+        y_copy(n, 1).wait_recv()
+        y_copy(n, 3).start()
 
     def share_done(n):
         for k in (2, 3):
-            y_copy(n // GROUPS, n % GROUPS, k).wait_recv()
+            y_copy(n, k).wait_recv()
 
     def kv_hand(h):
         return sent(kv.at[KV_OUT + h], kv.at[KV_IN + h + 1], kv_send_sem.at[h], kv_recv_sem.at[h], later)
@@ -326,9 +337,10 @@
         )
 
     def project_out(n):
-        h, g = n // GROUPS, n % GROUPS
-        rows = pl.ds(g * GROUP_ROWS, GROUP_ROWS)
-        wide = jnp.concatenate([attended[h + 1, g2, rows, :] for g2 in range(4)], axis=1)
+        share_done(n)
+        h, start, count = PIECES[n]
+        rows = pl.ds(start, count)
+        wide = jnp.concatenate([attended[h + 1, g, rows, :] for g in range(4)], axis=1)
         added = jnp.dot(wide, out_weights(h), preferred_element_type=F32)
         if h == 0:
             total[rows, :] = added
@@ -336,12 +348,11 @@
             total[rows, :] += added
         else:
             done = (total[rows, :] + added).astype(BF16)
-            start = g * GROUP_ROWS + BLOCK
-            if g < GROUPS - 1:
-                out[start : start + GROUP_ROWS, :] = done
+            if start + count < ROWS:
+                out[start + BLOCK : start + BLOCK + count, :] = done
             else:
-                out[start:ROWS, :] = done[: GROUP_ROWS - BLOCK]
-                out[0:BLOCK, :] = done[GROUP_ROWS - BLOCK :]
+                out[start + BLOCK : ROWS, :] = done[: count - BLOCK]
+                out[0:BLOCK, :] = done[count - BLOCK :]
 
     def swap_out_weights():
         @pl.when(moves)
@@ -358,47 +369,51 @@
 
     def catch_up():
         attend([BLOCKS + n for n in range(7)])
+        share(0)
 
     begin(0)
     token_copy.wait()
     normalize()
     relay(0)
+    begin(1)
+    begin(2)
     load_bank()
-    begin(1)
     relay_far(0)
+    cross(0)
     relay(1)
-    cross(0)
+    begin(3)
     for copy in bank_copies:
         copy.wait()
     arrived(0)
 
     after = {
-        (0, 0): [(relay_far, 1), (begin, 2)],
-        (0, 1): [(swap_out_weights,)],
-        (0, 2): [(relay, 2)],
-        (0, 3): [(cross, 1)],
-        (0, 4): [(arrived, 1), (project_queries, 0), (catch_up,), (relay_far, 2), (begin, 3)],
-        (0, 5): [(share, 0)],
-        (0, 6): [(cross, 2), (relay, 3)],
-        (0, 7): [(arrived, 2), (begin, 4)],
+        (0, 0): [(relay, 2)],
+        (0, 1): [(relay_far, 1), (swap_out_weights,)],
+        (0, 3): [(cross, 1), (begin, 4)],
+        (0, 4): [(arrived, 1), (project_queries, 0), (catch_up,), (relay_far, 2), (relay, 3)],
+        (0, 5): [(share, 1), (cross, 2)],
+        (0, 6): [(begin, 5), (arrived, 2)],
+        (0, 7): [(relay, 4)],
         (1, 0): [(relay_far, 3)],
-        (1, 1): [(relay, 4), (begin, 5), (share, 1)],
-        (1, 2): [(cross, 3)],
-        (1, 3): [(relay_far, 4), (share_relay, 0)],
-        (1, 4): [(relay, 5), (cross, 4), (begin, 6)],
-        (1, 5): [(share, 2)],
-        (1, 6): [(relay_far, 5)],
-        (1, 7): [(arrived, 3), (arrived, 4), (share_relay, 1), (project_queries, 1)],
-        (2, 0): [(cross, 5), (relay, 6)],
-        (2, 1): [(share, 3)],
-        (2, 2): [(relay_far, 6)],
-        (2, 3): [(arrived, 5), (share_relay, 2)],
-        (2, 4): [(cross, 6)],
-        (2, 5): [(share, 4)],
-        (2, 7): [(share_relay, 3)],
-        (3, 1): [(share, 5)],
-        (3, 5): [(share_relay, 4), (share, 6)],
-        (3, 7): [(arrived, 6)],
+        (1, 1): [(share, 2), (cross, 3), (share_relay, 0), (share_relay, 1)],
+        (1, 2): [(relay, 5), (relay_far, 4)],
+        (1, 3): [(arrived, 3), (begin, 6)],
+        (1, 4): [(cross, 4)],
+        (1, 5): [(share, 3), (relay_far, 5)],
+        (1, 6): [(arrived, 4)],
+        (1, 7): [(cross, 5), (project_queries, 1), (share_relay, 2)],
+        (2, 0): [(relay, 6), (arrived, 5)],
+        (2, 1): [(share, 4)],
+        (2, 2): [(share_relay, 3)],
+        (2, 4): [(relay_far, 6)],
+        (2, 5): [(share, 5)],
+        (2, 6): [(share_relay, 4), (cross, 6)],
+        (3, 0): [(arrived, 6)],
+        (3, 1): [(share, 6)],
+        (3, 2): [(share_relay, 5)],
+        (3, 5): [(share, 7)],
+        (3, 6): [(share_relay, 6)],
+        (3, 7): [(share, 8)],
     }
 
     def one_step(n, carry):
@@ -431,34 +446,28 @@
 
     kv_hand(HEADS - 1).wait_recv()
     attend([BLOCKS * HEADS + n for n in (13, 14, 15)])
-    share_done(0)
     project_out(0)
-    share(7)
-    share_done(1)
+    share(9)
     project_out(1)
-    share_relay(5)
-    share_done(2)
     project_out(2)
-    share_done(3)
+    share_relay(7)
     project_out(3)
-    share_relay(6)
-    share_done(4)
     project_out(4)
-    share_relay(7)
-    share_done(5)
+    share_relay(8)
     project_out(5)
-    share_done(6)
+    share_relay(9)
     project_out(6)
-    share_done(7)
     project_out(7)
+    project_out(8)
+    project_out(9)
 
     for r in range(O_ROUND + 1):
         for k in range(16):
             w_copy(r, k).wait_send()
         w_far_side(r).wait_send()
-    for n in range(HEADS * GROUPS):
+    for n in range(len(PIECES)):
         for k in range(4):
-            y_copy(n // GROUPS, n % GROUPS, k).wait_send()
+            y_copy(n, k).wait_send()
     for h in range(HEADS):
         kv_hand(h).wait_send()
 
@@ -468,7 +477,7 @@
 
 
 def local(tokens, neighbor_bank, slots, w_query, w_key, w_value, w_out):
-    hbm = pl.BlockSpec(memory_space=pl.ANY)
+    hbm = pl.BlockSpec(memory_space=pltpu.HBM)
     return pl.pallas_call(
         kernel,
         out_shape=jax.ShapeDtypeStruct((ROWS, HEADS * HEAD_DIM), BF16),
@@ -487,17 +496,17 @@
             pltpu.SemaphoreType.DMA((BLOCKS + 2,)),
             pltpu.SemaphoreType.DMA((O_ROUND + 1, 17)),
             pltpu.SemaphoreType.DMA((O_ROUND + 1, 17)),
-            pltpu.SemaphoreType.DMA((HEADS * GROUPS, 4)),
-            pltpu.SemaphoreType.DMA((HEADS * GROUPS, 4)),
+            pltpu.SemaphoreType.DMA((len(PIECES), 4)),
+            pltpu.SemaphoreType.DMA((len(PIECES), 4)),
             pltpu.SemaphoreType.DMA((HEADS,)),
             pltpu.SemaphoreType.DMA((HEADS,)),
             pltpu.SemaphoreType.DMA((2,)),
         ],
         compiler_params=pltpu.CompilerParams(
-            collective_id=0, has_side_effects=True, vmem_limit_bytes=64 * 1024 * 1024 - 512 * 1024
+            collective_id=0, has_side_effects=True, vmem_limit_bytes=52 * 1024 * 1024
         ),
         name="attention",
-    )(tokens, neighbor_bank, slots, w_query, w_key, w_value, w_out)
+    )(*[pltpu.with_memory_space_constraint(a, pltpu.HBM) for a in (tokens, neighbor_bank, slots, w_query, w_key, w_value, w_out)])
 
 
 def solution(mesh):

time: 89.9 us -> 72.5 us (0.81)
  Pallas kernels: 87.1 us -> 71.4 us
  local copies, waits for them, and re-layouts: 2.26 us -> 0.97 us
    pallas_call x1, Pallas kernels: 87.1 us -> 71.4 us  [local(): pl.pallas_call(kernel, out_shape=jax.ShapeDtypeStruct((ROWS, HEADS * HEAD...]
    unnamed x1, local copies, waits for them, and re-layouts: 2.26 us -> 0.97 us
where the time goes in v3:
time: 72.5 us; the launch traced here: 72.4 us
  Pallas kernels  71.4 us (98%)
  local copies, waits for them, and re-layouts  0.97 us (1%)
    pallas_call x1, Pallas kernels, local(): pl.pallas_call(kernel, out_shape=jax.ShapeDtypeStruct((ROWS, HEADS * HEAD...  71.4 us

profile of v3, /device:TPU:0, one launch (start us, length us, event | category | flops | bytes accessed | tf_op | source)
XLA Modules:
  0.0 72.4 jit_solution(13934040342888578739)
XLA Ops:
  0.0 71.4 %attention.1 = bf16[1024,512]{1,0:T(8,128)(2,1)S(1)} custom-call(bf16[1024,2048]{1,0:T(8,128)(2,1)} %tokens.1, bf16[16,256,2048]{2,1,0:T(8,128)(2,1)} %bank_hbm.1, s32[16]{0:T(128)} %slots.1, bf16[128,512]{1,0:T(8,128)(2,1)} %w_query.1, bf16[128,512]{1,0:T(8,128)(2,1)} %w_key.1, bf16[128,512]{1,0:T(8,128)(2,1)} %w_value.1, bf16[512,128]{1,0:T(8,128)(2,1)} %w_out.1), custom_call_target="tpu_custom_call" | custom-call | tf_op jit(solution)/shard_map/attention/pallas_call | solution.py:481
  71.4 1.0 %copy.9 = bf16[1024,512]{1,0:T(8,128)(2,1)} copy(bf16[1024,512]{1,0:T(8,128)(2,1)S(1)} %attention.1) | data formatting | bytes 2097152

commit v4 on v3

--- a/solution.py
+++ b/solution.py
@@ -16,24 +16,18 @@
 D = 2048
 ROWS = BLOCKS * BLOCK
 HEADS = 4
-PIECES = (
-    (0, 0, 256),
-    (0, 256, 256),
-    (0, 512, 512),
-    (1, 0, 512),
-    (1, 512, 512),
-    (2, 0, 512),
-    (2, 512, 512),
-    (3, 0, 512),
-    (3, 512, 256),
-    (3, 768, 256),
-)
+PIECES = tuple((h, start * BLOCK, count * BLOCK) for h in range(HEADS) for start, count in ((0, 7), (7, 4), (11, 5)))
+PIECES = PIECES[:-1] + ((3, 11 * BLOCK, 3 * BLOCK), (3, 14 * BLOCK, 2 * BLOCK))
 WIDTH = 2 * HEAD_DIM
 KV_ROUND = (0, 2, 3, 5)
 Q_ROUND = (1, 4)
 O_ROUND = 6
 KV_IN = 2 * BLOCKS
 KV_OUT = KV_IN + HEADS + 1
+SEND_OF = (0,) * 2 + (1,) * 2 + (2,) * 8 + (3,) * 5
+RECV_OF = (0, 1) + (2,) * 2 + (3,) * 8 + (4,) * 5
+STEP = 4
+STEPS = BLOCKS // STEP
 SCALE = 1.0 / math.sqrt(HEAD_DIM)
 BF16 = jnp.bfloat16
 F32 = jnp.float32
@@ -127,14 +121,14 @@
             parts = [(w_key, h * HEAD_DIM, 0, HEAD_DIM), (w_value, h * HEAD_DIM, HEAD_DIM, HEAD_DIM)]
         return [
             pltpu.make_async_copy(
-                w.at[:, pl.ds(start, width)], w_all.at[r, p, z, c, :, pl.ds(at, width)], stage_sem.at[r, n]
+                w.at[:, pl.ds(start, width)], w_all.at[r, p, z, c, :, pl.ds(at, width)], stage_sem.at[r]
             )
-            for n, (w, start, at, width) in enumerate(parts)
+            for w, start, at, width in parts
         ]
 
-    token_copy = pltpu.make_async_copy(tokens, normed, load_sem.at[BLOCKS])
-    bank_copies = [pltpu.make_async_copy(bank_hbm.at[b], bank.at[b], load_sem.at[b]) for b in range(BLOCKS)]
-    perm_local = pltpu.make_async_copy(w_out, o_all.at[p, z, c], load_sem.at[BLOCKS + 1])
+    token_copy = pltpu.make_async_copy(tokens, normed, load_sem.at[1])
+    bank_copies = [pltpu.make_async_copy(bank_hbm.at[b], bank.at[b], load_sem.at[0]) for b in range(BLOCKS)]
+    perm_local = pltpu.make_async_copy(w_out, o_all.at[p, z, c], load_sem.at[2])
     perm_dst = o_all.at[lax.div(perm_seq, 8), lax.rem(lax.div(perm_seq, 2), 4), lax.rem(perm_seq, 2)]
     perm_copy = sent(w_out, perm_dst, perm_sem.at[0], perm_sem.at[1], perm)
 
@@ -177,16 +171,26 @@
             15: (far, None, partner),
         }[k]
         ref = slab(r, *where, part)
-        return sent(ref, ref, w_send.at[r, k], w_recv.at[r, k], to)
+        return sent(ref, ref, w_send.at[r, SEND_OF[k]], w_recv.at[r, RECV_OF[k]], to)
+
+    def w_region(r, *where):
+        return w_all.at[(r, *where)] if r < O_ROUND else o_all.at[where]
 
     def w_far_side(r):
-        ref = w_all.at[r, 1 - p, :, c] if r < O_ROUND else o_all.at[1 - p, :, c]
-        return sent(ref, ref, w_send.at[r, 16], w_recv.at[r, 16], partner)
+        ref = w_region(r, 1 - p, slice(None), c)
+        return sent(ref, ref, w_send.at[r, SEND_OF[16]], w_recv.at[r, RECV_OF[16]], partner)
+
+    def w_taken(r, group, *where):
+        ref = w_region(r, *where)
+        sent(ref, ref, w_send.at[r, 0], w_recv.at[r, group], up).wait_recv()
+
+    def w_left(r, group, *where):
+        ref = w_region(r, *where)
+        sent(ref, ref, w_send.at[r, group], w_recv.at[r, 0], up).wait_send()
 
     def begin(r):
         if r < O_ROUND:
-            for copy in stage(r):
-                copy.wait()
+            pltpu.make_async_copy(w_query.at[:, pl.ds(0, WIDTH)], slab(r, p, z, c), stage_sem.at[r]).wait()
         else:
 
             @pl.when(moves)
@@ -201,27 +205,23 @@
             w_copy(r, k).start()
 
     def relay(r):
-        w_copy(r, 0).wait_recv()
+        w_taken(r, 0, p, z_prev, c)
         for k in (2, 10, 6, 7, 13):
             w_copy(r, k).start()
-        w_copy(r, 1).wait_recv()
+        w_taken(r, 1, p, z_next, c)
         for k in (3, 11, 8, 9, 14):
             w_copy(r, k).start()
 
     def relay_far(r):
-        w_copy(r, 2).wait_recv()
-        w_copy(r, 3).wait_recv()
+        w_taken(r, 2, p, z_far, c)
         w_copy(r, 15).start()
 
     def cross(r):
-        for k in range(4, 12):
-            w_copy(r, k).wait_recv()
+        w_taken(r, 3, 1 - p, slice(None), c)
         w_far_side(r).start()
 
     def arrived(r):
-        for k in range(12, 16):
-            w_copy(r, k).wait_recv()
-        w_far_side(r).wait_recv()
+        w_taken(r, 4, slice(None), slice(None), 1 - c)
 
     def y_copy(n, k):
         h, start, count = PIECES[n]
@@ -233,21 +233,30 @@
         }[k]
         rows = pl.ds(start, count) if part is None else pl.ds(start + part * (count // 2), count // 2)
         ref = attended.at[h + 1, whose, rows]
-        return sent(ref, ref, y_send.at[n, k], y_recv.at[n, k], to)
+        return sent(ref, ref, y_send.at[n], y_recv.at[n, min(k, 2)], to)
+
+    def y_taken(n, group, whose):
+        h, start, count = PIECES[n]
+        ref = attended.at[h + 1, whose, pl.ds(start, count)]
+        sent(ref, ref, y_send.at[n], y_recv.at[n, group], y_up).wait_recv()
 
     def share(n):
         for k in (0, 1):
             y_copy(n, k).start()
 
     def share_relay(n):
-        y_copy(n, 0).wait_recv()
+        y_taken(n, 0, y_prev)
         y_copy(n, 2).start()
-        y_copy(n, 1).wait_recv()
+        y_taken(n, 1, y_next)
         y_copy(n, 3).start()
 
     def share_done(n):
-        for k in (2, 3):
-            y_copy(n, k).wait_recv()
+        y_taken(n, 2, lax.rem(y + 2, 4))
+
+    def share_drain(n):
+        h, start, count = PIECES[n]
+        ref = attended.at[h + 1, pl.ds(0, 3), pl.ds(start, count)]
+        sent(ref, ref, y_send.at[n], y_recv.at[n, 0], y_up).wait_send()
 
     def kv_hand(h):
         return sent(kv.at[KV_OUT + h], kv.at[KV_IN + h + 1], kv_send_sem.at[h], kv_recv_sem.at[h], later)
@@ -312,18 +321,18 @@
         keep(tasks, mix(tasks, probs_of(scores), values))
 
     def step(h, i):
-        n = 8 * h + i
-        tasks = [2 * n + 13, 2 * n + 14]
+        tasks = [BLOCKS * h + STEP * i + BLOCKS - STEP - 1 + n for n in range(STEP)]
         scores, values = scores_of(tasks)
         probs = probs_of(scores)
-        first, second = lax.rem(2 * i + 15, BLOCKS), 2 * i
-        rows = jnp.concatenate([bank[slots[first]], bank[slots[second]]], axis=0)
-        pair = jnp.dot(rows, weights(h + lax.div(h + 1, 2)), preferred_element_type=F32).astype(BF16)
+        blocks = [lax.rem(STEP * i + BLOCKS - 1, BLOCKS)] + [STEP * i + n for n in range(STEP - 1)]
+        rows = jnp.concatenate([bank[slots[block]] for block in blocks], axis=0)
+        new = jnp.dot(rows, weights(h + lax.div(h + 1, 2)), preferred_element_type=F32).astype(BF16)
         mixed = mix(tasks, probs, values)
         own = lax.rem(h + 1, 2) * BLOCKS
-        later_step = lax.div(i + 7, 8)
-        kv[(1 - later_step) * (KV_OUT + h) + later_step * (own + first)] = pair[0:KEYS]
-        kv[own + second] = pair[KEYS : 2 * KEYS]
+        kept = lax.div(i + STEPS - 1, STEPS)
+        kv[(1 - kept) * (KV_OUT + h) + kept * (own + blocks[0])] = new[0:KEYS]
+        for n in range(1, STEP):
+            kv[own + blocks[n]] = new[n * KEYS : (n + 1) * KEYS]
         keep(tasks, mixed)
 
     def out_weights(h):
@@ -371,6 +380,12 @@
         attend([BLOCKS + n for n in range(7)])
         share(0)
 
+    def drain(r):
+        w_left(r, 0, slice(None), z, c)
+        w_left(r, 1, p, z, c)
+        w_left(r, 2, 1 - p, slice(None), c)
+        w_left(r, 3, slice(None), slice(None), c)
+
     begin(0)
     token_copy.wait()
     normalize()
@@ -379,97 +394,91 @@
     begin(2)
     load_bank()
     relay_far(0)
+    relay(1)
     cross(0)
-    relay(1)
+    relay(2)
     begin(3)
-    for copy in bank_copies:
-        copy.wait()
+    pltpu.make_async_copy(bank_hbm, bank, load_sem.at[0]).wait()
     arrived(0)
 
     after = {
-        (0, 0): [(relay, 2)],
-        (0, 1): [(relay_far, 1), (swap_out_weights,)],
-        (0, 3): [(cross, 1), (begin, 4)],
-        (0, 4): [(arrived, 1), (project_queries, 0), (catch_up,), (relay_far, 2), (relay, 3)],
-        (0, 5): [(share, 1), (cross, 2)],
-        (0, 6): [(begin, 5), (arrived, 2)],
-        (0, 7): [(relay, 4)],
-        (1, 0): [(relay_far, 3)],
-        (1, 1): [(share, 2), (cross, 3), (share_relay, 0), (share_relay, 1)],
-        (1, 2): [(relay, 5), (relay_far, 4)],
-        (1, 3): [(arrived, 3), (begin, 6)],
-        (1, 4): [(cross, 4)],
-        (1, 5): [(share, 3), (relay_far, 5)],
-        (1, 6): [(arrived, 4)],
-        (1, 7): [(cross, 5), (project_queries, 1), (share_relay, 2)],
-        (2, 0): [(relay, 6), (arrived, 5)],
-        (2, 1): [(share, 4)],
-        (2, 2): [(share_relay, 3)],
-        (2, 4): [(relay_far, 6)],
-        (2, 5): [(share, 5)],
-        (2, 6): [(share_relay, 4), (cross, 6)],
-        (3, 0): [(arrived, 6)],
-        (3, 1): [(share, 6)],
-        (3, 2): [(share_relay, 5)],
-        (3, 5): [(share, 7)],
-        (3, 6): [(share_relay, 6)],
-        (3, 7): [(share, 8)],
+        0: [(relay_far, 1)],
+        1: [(cross, 1), (swap_out_weights,), (begin, 4)],
+        2: [(arrived, 1), (project_queries, 0), (catch_up,), (relay_far, 2), (cross, 2), (relay, 3)],
+        3: [(share, 1), (arrived, 2), (begin, 5)],
+        4: [(relay, 4)],
+        5: [(share, 2), (share_relay, 0), (relay_far, 3)],
+        6: [(share, 3), (cross, 3), (relay, 5), (share_relay, 1), (begin, 6)],
+        7: [(share, 4), (relay_far, 4), (cross, 4), (arrived, 3)],
+        8: [(share_relay, 2), (arrived, 4), (project_queries, 1), (relay_far, 5)],
+        9: [(share, 5), (cross, 5), (relay, 6)],
+        10: [(share, 6), (share_relay, 3)],
+        11: [(share, 7), (arrived, 5), (share_relay, 4)],
+        12: [(share_relay, 5), (relay_far, 6)],
+        13: [(share, 8), (cross, 6)],
+        14: [(share, 9), (share_relay, 6)],
+        15: [(share, 10)],
     }
 
     def one_step(n, carry):
-        h, i = lax.div(n, 8), lax.rem(n, 8)
+        h, i = lax.div(n, STEPS), lax.rem(n, STEPS)
         step(h, i)
 
-        @pl.when(i == 1)
+        for head in range(HEADS):
+
+            @pl.when(h == head)
+            def _(head=head):
+                for at in range(STEPS):
+
+                    @pl.when(i == at)
+                    def _(at=at):
+                        for action, *rest in after[STEPS * head + at]:
+                            action(*rest)
+
+        @pl.when(i == 0)
         def _():
             kv_hand(h).start()
 
-        @pl.when(jnp.logical_and(i == 0, h > 0))
-        def _():
-            kv_hand(h - 1).wait_recv()
-
-        for head in range(HEADS):
-
-            @pl.when(h == head)
-            def _(head=head):
-                for (at, place_in), actions in after.items():
-                    if at == head:
-
-                        @pl.when(i == place_in)
-                        def _(actions=actions):
-                            for action, *rest in actions:
-                                action(*rest)
+            @pl.when(h > 0)
+            def _():
+                kv_hand(h - 1).wait_recv()
 
         return carry
 
-    lax.fori_loop(0, 8 * HEADS, one_step, 0)
+    lax.fori_loop(0, STEPS * HEADS, one_step, 0)
 
     kv_hand(HEADS - 1).wait_recv()
-    attend([BLOCKS * HEADS + n for n in (13, 14, 15)])
+    attend([BLOCKS * HEADS + n for n in (11, 12, 13, 14, 15)])
+    arrived(6)
     project_out(0)
-    share(9)
+    share(11)
+    share(12)
+    share_relay(7)
     project_out(1)
     project_out(2)
-    share_relay(7)
     project_out(3)
+    share_relay(8)
     project_out(4)
-    share_relay(8)
     project_out(5)
+    for r in range(O_ROUND + 1):
+        drain(r)
     share_relay(9)
     project_out(6)
+    share_relay(10)
+    share_relay(11)
+    share_relay(12)
     project_out(7)
     project_out(8)
-    project_out(9)
-
-    for r in range(O_ROUND + 1):
-        for k in range(16):
-            w_copy(r, k).wait_send()
-        w_far_side(r).wait_send()
-    for n in range(len(PIECES)):
-        for k in range(4):
-            y_copy(n, k).wait_send()
+    for n in range(8):
+        share_drain(n)
     for h in range(HEADS):
         kv_hand(h).wait_send()
+    project_out(9)
+    project_out(10)
+    project_out(11)
+    project_out(12)
+    for n in range(8, len(PIECES)):
+        share_drain(n)
 
     @pl.when(moves)
     def _():
@@ -492,12 +501,12 @@
             pltpu.VMEM((KV_OUT + HEADS, KEYS, WIDTH), BF16),
             pltpu.VMEM((HEADS + 1, 4, ROWS, HEAD_DIM), BF16),
             pltpu.VMEM((ROWS, 512), F32),
-            pltpu.SemaphoreType.DMA((O_ROUND, 2)),
-            pltpu.SemaphoreType.DMA((BLOCKS + 2,)),
-            pltpu.SemaphoreType.DMA((O_ROUND + 1, 17)),
-            pltpu.SemaphoreType.DMA((O_ROUND + 1, 17)),
-            pltpu.SemaphoreType.DMA((len(PIECES), 4)),
-            pltpu.SemaphoreType.DMA((len(PIECES), 4)),
+            pltpu.SemaphoreType.DMA((O_ROUND,)),
+            pltpu.SemaphoreType.DMA((3,)),
+            pltpu.SemaphoreType.DMA((O_ROUND + 1, 4)),
+            pltpu.SemaphoreType.DMA((O_ROUND + 1, 5)),
+            pltpu.SemaphoreType.DMA((len(PIECES),)),
+            pltpu.SemaphoreType.DMA((len(PIECES), 3)),
             pltpu.SemaphoreType.DMA((HEADS,)),
             pltpu.SemaphoreType.DMA((HEADS,)),
             pltpu.SemaphoreType.DMA((2,)),

time: 72.5 us -> 66.4 us (0.916); the launches traced: 72.4 us -> 65.1 us
  Pallas kernels: 71.4 us -> 64.2 us
    pallas_call x1, Pallas kernels: 71.4 us -> 64.2 us  [local(): pl.pallas_call(kernel, out_shape=jax.ShapeDtypeStruct((ROWS, HEADS * HEAD...]
where the time goes in v4:
time: 66.4 us; the launch traced here: 65.1 us
  Pallas kernels  64.2 us (97%)
  local copies, waits for them, and re-layouts  0.97 us (1%)
    pallas_call x1, Pallas kernels, local(): pl.pallas_call(kernel, out_shape=jax.ShapeDtypeStruct((ROWS, HEADS * HEAD...  64.2 us

profile of v4, /device:TPU:0, one launch (start us, length us, event | category | flops | bytes accessed | tf_op | source)
XLA Modules:
  0.0 65.1 jit_solution(9950631072934624727)
XLA Ops:
  0.0 64.2 %attention.1 = bf16[1024,512]{1,0:T(8,128)(2,1)S(1)} custom-call(bf16[1024,2048]{1,0:T(8,128)(2,1)} %tokens.1, bf16[16,256,2048]{2,1,0:T(8,128)(2,1)} %bank_hbm.1, s32[16]{0:T(128)} %slots.1, bf16[128,512]{1,0:T(8,128)(2,1)} %w_query.1, bf16[128,512]{1,0:T(8,128)(2,1)} %w_key.1, bf16[128,512]{1,0:T(8,128)(2,1)} %w_value.1, bf16[512,128]{1,0:T(8,128)(2,1)} %w_out.1), custom_call_target="tpu_custom_call" | custom-call | tf_op jit(solution)/shard_map/attention/pallas_call | solution.py:490
  64.2 1.0 %copy.9 = bf16[1024,512]{1,0:T(8,128)(2,1)} copy(bf16[1024,512]{1,0:T(8,128)(2,1)S(1)} %attention.1) | data formatting | bytes 2097152

commit v5 on v4

--- a/solution.py
+++ b/solution.py
@@ -171,22 +171,22 @@
             15: (far, None, partner),
         }[k]
         ref = slab(r, *where, part)
-        return sent(ref, ref, w_send.at[r, SEND_OF[k]], w_recv.at[r, RECV_OF[k]], to)
+        return sent(ref, ref, w_send.at[r // O_ROUND, SEND_OF[k]], w_recv.at[r, RECV_OF[k]], to)
 
     def w_region(r, *where):
         return w_all.at[(r, *where)] if r < O_ROUND else o_all.at[where]
 
     def w_far_side(r):
         ref = w_region(r, 1 - p, slice(None), c)
-        return sent(ref, ref, w_send.at[r, SEND_OF[16]], w_recv.at[r, RECV_OF[16]], partner)
+        return sent(ref, ref, w_send.at[r // O_ROUND, SEND_OF[16]], w_recv.at[r, RECV_OF[16]], partner)
 
     def w_taken(r, group, *where):
         ref = w_region(r, *where)
-        sent(ref, ref, w_send.at[r, 0], w_recv.at[r, group], up).wait_recv()
-
-    def w_left(r, group, *where):
-        ref = w_region(r, *where)
-        sent(ref, ref, w_send.at[r, group], w_recv.at[r, 0], up).wait_send()
+        sent(ref, ref, w_send.at[0, 0], w_recv.at[r, group], up).wait_recv()
+
+    def w_left(group, *where):
+        for last, ref in enumerate((w_all.at[(slice(None), *where)], o_all.at[where])):
+            sent(ref, ref, w_send.at[last, group], w_recv.at[0, 0], up).wait_send()
 
     def begin(r):
         if r < O_ROUND:
@@ -233,12 +233,12 @@
         }[k]
         rows = pl.ds(start, count) if part is None else pl.ds(start + part * (count // 2), count // 2)
         ref = attended.at[h + 1, whose, rows]
-        return sent(ref, ref, y_send.at[n], y_recv.at[n, min(k, 2)], to)
+        return sent(ref, ref, y_send.at[0], y_recv.at[n, min(k, 2)], to)
 
     def y_taken(n, group, whose):
         h, start, count = PIECES[n]
         ref = attended.at[h + 1, whose, pl.ds(start, count)]
-        sent(ref, ref, y_send.at[n], y_recv.at[n, group], y_up).wait_recv()
+        sent(ref, ref, y_send.at[0], y_recv.at[n, group], y_up).wait_recv()
 
     def share(n):
         for k in (0, 1):
@@ -253,13 +253,12 @@
     def share_done(n):
         y_taken(n, 2, lax.rem(y + 2, 4))
 
-    def share_drain(n):
-        h, start, count = PIECES[n]
-        ref = attended.at[h + 1, pl.ds(0, 3), pl.ds(start, count)]
-        sent(ref, ref, y_send.at[n], y_recv.at[n, 0], y_up).wait_send()
+    def share_drain():
+        ref = attended.at[pl.ds(1, HEADS), pl.ds(0, 3)]
+        sent(ref, ref, y_send.at[0], y_recv.at[0, 0], y_up).wait_send()
 
     def kv_hand(h):
-        return sent(kv.at[KV_OUT + h], kv.at[KV_IN + h + 1], kv_send_sem.at[h], kv_recv_sem.at[h], later)
+        return sent(kv.at[KV_OUT + h], kv.at[KV_IN + h + 1], kv_send_sem.at[0], kv_recv_sem.at[h], later)
 
     def normalize():
         def body(i, carry):
@@ -380,11 +379,13 @@
         attend([BLOCKS + n for n in range(7)])
         share(0)
 
-    def drain(r):
-        w_left(r, 0, slice(None), z, c)
-        w_left(r, 1, p, z, c)
-        w_left(r, 2, 1 - p, slice(None), c)
-        w_left(r, 3, slice(None), slice(None), c)
+    def drain():
+        w_left(0, slice(None), z, c)
+        w_left(1, p, z, c)
+        w_left(2, 1 - p, slice(None), c)
+        w_left(3, slice(None), slice(None), c)
+        ref = kv.at[pl.ds(KV_OUT, HEADS)]
+        sent(ref, ref, kv_send_sem.at[0], kv_recv_sem.at[0], later).wait_send()
 
     begin(0)
     token_copy.wait()
@@ -460,8 +461,7 @@
     share_relay(8)
     project_out(4)
     project_out(5)
-    for r in range(O_ROUND + 1):
-        drain(r)
+    drain()
     share_relay(9)
     project_out(6)
     share_relay(10)
@@ -469,16 +469,11 @@
     share_relay(12)
     project_out(7)
     project_out(8)
-    for n in range(8):
-        share_drain(n)
-    for h in range(HEADS):
-        kv_hand(h).wait_send()
     project_out(9)
     project_out(10)
     project_out(11)
     project_out(12)
-    for n in range(8, len(PIECES)):
-        share_drain(n)
+    share_drain()
 
     @pl.when(moves)
     def _():
@@ -503,11 +498,11 @@
             pltpu.VMEM((ROWS, 512), F32),
             pltpu.SemaphoreType.DMA((O_ROUND,)),
             pltpu.SemaphoreType.DMA((3,)),
-            pltpu.SemaphoreType.DMA((O_ROUND + 1, 4)),
+            pltpu.SemaphoreType.DMA((2, 4)),
             pltpu.SemaphoreType.DMA((O_ROUND + 1, 5)),
-            pltpu.SemaphoreType.DMA((len(PIECES),)),
+            pltpu.SemaphoreType.DMA((1,)),
             pltpu.SemaphoreType.DMA((len(PIECES), 3)),
-            pltpu.SemaphoreType.DMA((HEADS,)),
+            pltpu.SemaphoreType.DMA((1,)),
             pltpu.SemaphoreType.DMA((HEADS,)),
             pltpu.SemaphoreType.DMA((2,)),
         ],

time: 66.4 us -> 66.1 us (level)
  no operation moved by 1% of the time
where the time goes in v5:
time: 66.1 us; the launch traced here: 64.8 us
  Pallas kernels  63.8 us (97%)
  local copies, waits for them, and re-layouts  0.97 us (1%)
    pallas_call x1, Pallas kernels, local(): pl.pallas_call(kernel, out_shape=jax.ShapeDtypeStruct((ROWS, HEADS * HEAD...  63.8 us

profile of v5, /device:TPU:0, one launch (start us, length us, event | category | flops | bytes accessed | tf_op | source)
XLA Modules:
  0.0 64.8 jit_solution(18389631490197255593)
XLA Ops:
  0.0 63.8 %attention.1 = bf16[1024,512]{1,0:T(8,128)(2,1)S(1)} custom-call(bf16[1024,2048]{1,0:T(8,128)(2,1)} %tokens.1, bf16[16,256,2048]{2,1,0:T(8,128)(2,1)} %bank_hbm.1, s32[16]{0:T(128)} %slots.1, bf16[128,512]{1,0:T(8,128)(2,1)} %w_query.1, bf16[128,512]{1,0:T(8,128)(2,1)} %w_key.1, bf16[128,512]{1,0:T(8,128)(2,1)} %w_value.1, bf16[512,128]{1,0:T(8,128)(2,1)} %w_out.1), custom_call_target="tpu_custom_call" | custom-call | tf_op jit(solution)/shard_map/attention/pallas_call | solution.py:485
  63.8 1.0 %copy.9 = bf16[1024,512]{1,0:T(8,128)(2,1)} copy(bf16[1024,512]{1,0:T(8,128)(2,1)S(1)} %attention.1) | data formatting | bytes 2097152
